TPU v7x, 256 devices: a whole 4x4x8 slice. The times are simulated.
256 devices in a mesh: freq: 32 (over z_hi, y, x), slab: 8 (over z_lo, core).
Axes of the slice: x: 4, y: 4, z: 8 (z_hi: 2, z_lo: 4; z = z_hi * 4 + z_lo), core: 2. Of those that a mesh axis runs over, the one named last changes fastest.
Arguments:
- log_conductivity: float32 [40, 32, 128], P('slab'), may hold values from -1 to 1
- omega: float32 [32], P('freq'), may hold values from 0.1 to 2
- sources: float32 [32, 2, 2, 3, 40, 32, 128], P('freq', None, None, None, 'slab'), may hold values from -8 to 8
- receivers: int32 [1024], P('slab'), may hold values from 0 to 20479
- observed: float32 [32, 2, 2, 3, 1024], P('freq', None, None, None, 'slab'), may hold values from -2.4 to 2.4
- data_weight: float32 [32, 2, 3, 1024], P('freq', None, None, 'slab'), may hold values from 3 to 30
- prior_gradient: float32 [40, 32, 128], P('slab', 'freq'), may hold values from -6 to 6
- prior_direction: float32 [40, 32, 128], P('slab', 'freq'), may hold values from -6 to 6
- step_length: float32 [1], replicated, may hold values from 0.2 to 0.6
Outputs:
- unit_direction: float32 [40, 32, 128], P('slab', 'freq')
- trial_model: float32 [40, 32, 128], P('slab')
Inputs may be any that keep to these rules, and one draw needn't show every extreme that they name: Each block of 128 receivers belongs to one slab of 5 layers, slabs in order; an entry is z * 32 * 128 + y * 128 + x within its slab; cells may repeat.
All inputs are finite; a program needn't handle non-finite values.
Results may differ from a plain program's by a relative error of at most 0.0011.
Values sent between devices are 32-bit elements; how exact they have to be, the bound alone decides.
A program may use at most 128 MiB of HBM per device.

v0:
```python
import functools

import jax
import jax.numpy as jnp
from jax import lax
from jax.experimental import pallas as pl
from jax.experimental.pallas import tpu as pltpu
from jax.sharding import PartitionSpec as P


MESH = pl.DeviceIdType.MESH
epsilon = 1e-06
F32 = jnp.float32
BF16 = jnp.bfloat16
LOW = 3
HIGH = 4


def cmul(a, b):
    return a[0] * b[0] - a[1] * b[1], a[0] * b[1] + a[1] * b[0]


def cadd(a, b):
    return a[0] + b[0], a[1] + b[1]


def csub(a, b):
    return a[0] - b[0], a[1] - b[1]


def cdiv(a, b):
    modulus = b[0] * b[0] + b[1] * b[1]
    return (a[0] * b[0] + a[1] * b[1]) / modulus, (a[1] * b[0] - a[0] * b[1]) / modulus


def square_poly(p):
    out = [None] * (2 * len(p) - 1)
    for i in range(len(p)):
        for j in range(i, len(p)):
            term = cmul(p[i], p[j])
            if j > i:
                term = (term[0] + term[0], term[1] + term[1])
            out[i + j] = term if out[i + j] is None else cadd(out[i + j], term)
    return out


def against(poly, moments):
    total = None
    for c, m in zip(poly, moments):
        term = cmul(c, m)
        total = term if total is None else cadd(total, term)
    return total


def coefficients(moments):
    steps = [csub(a, b) for a, b in zip(moments, moments[1:])]
    one = (jnp.ones_like(moments[0][0]), jnp.zeros_like(moments[0][0]))
    residual, direction, rho = [one], [one], moments[0]
    solution = []
    for iteration in range(4):
        alpha = cdiv(rho, against(square_poly(direction), steps))
        moved = [cmul(alpha, c) for c in direction]
        solution = [cadd(a, b) for a, b in zip(solution, moved)] + moved[len(solution) :]
        if iteration < 3:
            grown = [csub(r, m) for r, m in zip(residual, moved)]
            grown.append((jnp.zeros_like(rho[0]), jnp.zeros_like(rho[0])))
            residual = [grown[0]] + [cadd(grown[k + 1], moved[k]) for k in range(len(moved))]
            rho_next = against(square_poly(residual), moments)
            beta = cdiv(rho_next, rho)
            direction = [
                cadd(residual[k], cmul(beta, direction[k])) for k in range(len(direction))
            ] + [residual[-1]]
            rho = rho_next
    return [(c[0] * 6.0 ** -(k + 1), c[1] * 6.0 ** -(k + 1)) for k, c in enumerate(solution)]


def split3(x):
    high = x.astype(BF16)
    rest = x - high.astype(F32)
    mid = rest.astype(BF16)
    low = (rest - mid.astype(F32)).astype(BF16)
    return high, mid, low


def kernel(
    layers,
    slabs,
    positions,
    omega_ref,
    step_ref,
    logc_ref,
    src_ref,
    rec_ref,
    obs_ref,
    wt_ref,
    pg_ref,
    pd_ref,
    dir_ref,
    trial_ref,
    v0,
    v1,
    v2,
    v3,
    field,
    kap,
    lcg,
    recs,
    data,
    allred,
    prior_pair,
    prior_all,
    grad,
    grad_src,
    grad_in,
    grad_pair,
    grad_all,
    unit,
    natural,
    load_sem,
    near_send,
    near_recv,
    data_send,
    data_recv,
    ar_send,
    ar_recv,
    pair_send,
    pair_recv,
    fan_send,
    fan_recv,
):
    freq = lax.axis_index("freq")
    slab = lax.axis_index("slab")
    half = freq // positions
    place = freq % positions
    base = half * positions
    partner = (1 - half) * positions + place
    own_lo, own_hi = LOW, LOW + layers
    total_layers = LOW + layers + HIGH

    def remote(src, dst, send, recv, to):
        return pltpu.make_async_remote_copy(
            src_ref=src, dst_ref=dst, send_sem=send, recv_sem=recv, device_id=to, device_id_type=MESH
        )

    barrier = pltpu.get_barrier_semaphore()
    for d in range(1, slabs):
        to = (freq, (slab + d) % slabs)
        pl.semaphore_signal(barrier, inc=1, device_id=to, device_id_type=MESH)
    for d in range(1, positions):
        to = (base + (place + d) % positions, slab)
        pl.semaphore_signal(barrier, inc=1, device_id=to, device_id_type=MESH)
    pl.semaphore_signal(barrier, inc=1, device_id=(partner, slab), device_id_type=MESH)

    load = pltpu.make_async_copy(
        src_ref, v0.at[:, pl.ds(own_lo, layers), pl.ds(8, 32), :], load_sem
    )
    load.start()

    edge = jnp.zeros((12, total_layers, 8, 128), F32)
    for v in (v0, v1, v2, v3):
        v[:, :, 0:8, :] = edge
        v[:, :, 40:48, :] = edge
    has_below = slab > 0
    has_above = slab < slabs - 1

    @pl.when(slab == 0)
    def _():
        v0[:, 0:LOW, 8:40, :] = jnp.zeros((12, LOW, 32, 128), F32)
        lcg[0:2] = jnp.zeros((2, 32, 128), F32)
        recs[0] = jnp.zeros((1, 128), jnp.int32)
        data[0] = jnp.zeros((12, 128), F32)

    @pl.when(slab == slabs - 1)
    def _():
        v0[:, own_hi:total_layers, 8:40, :] = jnp.zeros((12, HIGH, 32, 128), F32)
        lcg[2:5] = jnp.zeros((3, 32, 128), F32)
        recs[2] = jnp.zeros((1, 128), jnp.int32)
        data[2] = jnp.zeros((12, 128), F32)

    omega = omega_ref[0]
    kap[own_lo:own_hi] = omega * jnp.exp(logc_ref[...])
    for l in range(layers):
        prior_pair[half, 0, l : l + 1, :] = pg_ref[l]
        prior_pair[half, 1, l : l + 1, :] = pd_ref[l]
    recs[1] = rec_ref[...]

    load.wait()
    pl.semaphore_wait(barrier, slabs + positions - 1)

    rows = pl.ds(8, 32)
    below_to = (freq, lax.max(slab - 1, 0))
    above_to = (freq, lax.min(slab + 1, slabs - 1))
    upward = []
    downward = []
    upward.append((rec_ref, recs.at[0]))
    downward.append((rec_ref, recs.at[2]))
    upward.append((logc_ref.at[pl.ds(layers - 2, 2)], lcg.at[pl.ds(0, 2)]))
    downward.append((logc_ref.at[pl.ds(0, 3)], lcg.at[pl.ds(2, 3)]))
    for k in range(HIGH):
        if k < LOW:
            upward.append(
                (v0.at[:, own_hi - 1 - k, rows, :], v0.at[:, own_lo - 1 - k, rows, :])
            )
        downward.append((v0.at[:, own_lo + k, rows, :], v0.at[:, own_hi + k, rows, :]))
    ups = [
        remote(s, d, near_send.at[0, n], near_recv.at[0, n], above_to)
        for n, (s, d) in enumerate(upward)
    ]
    downs = [
        remote(s, d, near_send.at[1, n], near_recv.at[1, n], below_to)
        for n, (s, d) in enumerate(downward)
    ]

    @pl.when(has_above)
    def _():
        for c in ups:
            c.start()

    @pl.when(has_below)
    def _():
        for c in downs:
            c.start()

    prior_copy = remote(
        prior_pair.at[half], prior_pair.at[half], pair_send.at[0], pair_recv.at[0], (partner, slab)
    )
    prior_copy.start()

    def arrived(n):
        if n < len(ups):

            @pl.when(has_below)
            def _():
                ups[n].wait_recv()

        @pl.when(has_above)
        def _():
            downs[n].wait_recv()

    lane = lax.broadcasted_iota(jnp.int32, (32, 128), 1)
    first_lane, last_lane = lane == 0, lane == 127
    alive_low = jnp.where(slab == 0, 0.0, 1.0).astype(F32)
    alive_high = jnp.where(slab == slabs - 1, 0.0, 1.0).astype(F32)

    def step(src, dst, l, mask=None):
        coupling = kap[l]

        def around(p):
            here = src[p, l, 8:40, :]
            total = src[p, l - 1, 8:40, :] + src[p, l + 1, 8:40, :]
            total = total + (src[p, l, 7:39, :] + src[p, l, 9:41, :])
            left = jnp.where(first_lane, 0.0, pltpu.roll(here, 1, 1))
            right = jnp.where(last_lane, 0.0, pltpu.roll(here, 127, 1))
            return here, total + (left + right)

        for pol in range(2):
            for comp in range(3):
                p = pol * 6 + comp
                re, around_re = around(p)
                im, around_im = around(p + 3)
                new_re = around_re + coupling * im
                new_im = around_im - coupling * re
                if mask is not None:
                    new_re, new_im = mask * new_re, mask * new_im
                dst[p, l, 8:40, :] = new_re
                dst[p + 3, l, 8:40, :] = new_im

    def sweep(src, dst, lo, hi, mask=None):
        def body(l, carry):
            step(src, dst, l, mask)
            return carry

        lax.fori_loop(lo, hi, body, 0)

    def both(src, dst, low, high, ghost):
        def body(n, carry):
            mask = jnp.where(n == 0, alive_low, alive_high) if ghost else None
            step(src, dst, low + n * (high - low), mask)
            return carry

        lax.fori_loop(0, 2, body, 0)

    def moment_row(v_list):
        a, b, c, e = v_list
        sums = []
        lane8 = lax.broadcasted_iota(jnp.int32, (8, 128), 1)
        last8 = lane8 == 127
        for pol in range(2):

            def body(l, acc):
                acc = list(acc)

                def add(k, value):
                    acc[k] = acc[k] + value

                for comp in range(3):
                    p = pol * 6 + comp
                    for r in range(4):
                        y = 8 + 8 * r
                        vs = [(v[p, l, y : y + 8, :], v[p + 3, l, y : y + 8, :]) for v in v_list]
                        for k in range(4):
                            re, im = vs[k]
                            add(4 * k, (re - im) * (re + im))
                            add(4 * k + 1, re * im)
                        coupling = kap[l, 8 * r : 8 * r + 8, :]
                        halves = []
                        for q in (p, p + 3):
                            here = e[q, l, y : y + 8, :]
                            right = jnp.where(last8, 0.0, pltpu.roll(here, 127, 1))
                            more = e[q, l + 1, y : y + 8, :] + e[q, l, y + 1 : y + 9, :] + right
                            halves.append(more + more)
                        re, im = vs[3]
                        after = (halves[0] + coupling * im, halves[1] - coupling * re)
                        pairs = [(vs[0], vs[1]), (vs[1], vs[2]), (vs[2], vs[3]), (vs[3], after)]
                        for k, (u, w) in enumerate(pairs):
                            add(4 * k + 2, u[0] * w[0] - u[1] * w[1])
                            add(4 * k + 3, u[0] * w[1] + u[1] * w[0])
                return tuple(acc)

            zero = jnp.zeros((8, 128), F32)
            sums += list(lax.fori_loop(own_lo, own_hi, body, (zero,) * 16))
        lanes = lax.broadcasted_iota(jnp.int32, (1, 128), 1)
        row = jnp.zeros((1, 128), F32)
        for n, s in enumerate(sums):
            line = jnp.sum(s, axis=0, keepdims=True)
            row = row + jnp.where(lanes == n, jnp.sum(line, axis=1, keepdims=True), 0.0)
        return row

    def slab_total(n, row):
        allred[n, slab] = row
        copies = []
        for d in range(1, slabs):
            to = (freq, (slab + d) % slabs)
            copies.append(
                remote(
                    allred.at[n, slab],
                    allred.at[n, slab],
                    ar_send.at[n, d],
                    ar_recv.at[n, slab],
                    to,
                )
            )
        for c in copies:
            c.start()
        for d in range(1, slabs):
            other = (slab + d) % slabs
            remote(
                allred.at[n, other],
                allred.at[n, other],
                ar_send.at[n, d],
                ar_recv.at[n, other],
                (freq, other),
            ).wait_recv()
        total = allred[n, 0]
        for j in range(1, slabs):
            total = total + allred[n, j]
        return total, copies

    def solve_coefficients(row):
        lanes = lax.broadcasted_iota(jnp.int32, (1, 128), 1)

        def pick(n):
            return jnp.sum(jnp.where(lanes == n, row, 0.0), axis=1, keepdims=True)

        found = []
        for pol in range(2):
            moments = []
            for k in range(8):
                re = pick(16 * pol + 2 * k) * 6.0**-k
                im = pick(16 * pol + 2 * k + 1) * 6.0**-k
                if k % 2 == 0:
                    im = im + im
                moments.append((re, im))
            most = None
            for m in moments:
                size = jnp.maximum(jnp.abs(m[0]), jnp.abs(m[1]))
                most = size if most is None else jnp.maximum(most, size)
            moments = [(m[0] / most, m[1] / most) for m in moments]
            found.append(coefficients(moments))
        return found

    def combined(coefs, pol, comp, l, y):
        p = pol * 6 + comp
        re = im = None
        for (cr, ci), v in zip(coefs[pol], (v0, v1, v2, v3)):
            a, b = v[p, l, y : y + 8, :], v[p + 3, l, y : y + 8, :]
            tr, ti = cr * a - ci * b, cr * b + ci * a
            re, im = (tr, ti) if re is None else (re + tr, im + ti)
        return re, im

    sweep(v0, v1, own_lo + 1, own_hi - 1)
    step(v1, v2, own_lo + 2)
    arrived(0)
    arrived(1)
    kap[1:3] = omega * jnp.exp(lcg[0:2])
    kap[own_hi : own_hi + 3] = omega * jnp.exp(lcg[2:5])
    arrived(2)
    both(v0, v1, own_lo, own_hi - 1, False)
    both(v1, v2, own_lo + 1, own_hi - 2, False)
    step(v2, v3, own_lo + 2)
    arrived(3)
    both(v0, v1, own_lo - 1, own_hi, True)
    both(v1, v2, own_lo, own_hi - 1, False)
    both(v2, v3, own_lo + 1, own_hi - 2, False)
    arrived(4)
    both(v0, v1, own_lo - 2, own_hi + 1, True)
    both(v1, v2, own_lo - 1, own_hi, True)
    both(v2, v3, own_lo, own_hi - 1, False)
    arrived(5)
    step(v0, v1, own_hi + 2, alive_high)
    step(v1, v2, own_hi + 1, alive_high)
    step(v2, v3, own_hi, alive_high)
    row, sent_a = slab_total(0, moment_row((v0, v1, v2, v3)))
    coefs = solve_coefficients(row)

    def write_field(l, carry):
        for pol in range(2):
            for comp in range(3):
                for r in range(4):
                    re, im = combined(coefs, pol, comp, l, 8 + 8 * r)
                    field[pol * 6 + comp, l - own_lo, 8 * r : 8 * r + 8, :] = re
                    field[pol * 6 + 3 + comp, l - own_lo, 8 * r : 8 * r + 8, :] = im
        return carry

    lax.fori_loop(own_lo, own_hi, write_field, 0)

    def onehots(n):
        where = recs[n]
        return where // 128, where % 128

    wide = 32 * layers
    line_of, lane_of = onehots(1)
    column = (lax.broadcasted_iota(jnp.int32, (128, 128), 0) == lane_of).astype(F32)
    column = column.astype(BF16)
    taller = jnp.concatenate([column] * 3, axis=0)
    at_row = lax.broadcasted_iota(jnp.int32, (wide, 128), 0) == line_of
    for pol in range(2):
        for ri in range(2):
            for comp in range(3):
                p = pol * 6 + ri * 3 + comp
                plane = field[p].reshape(wide, 128)
                parts = jnp.concatenate(split3(plane), axis=1)
                seen = jnp.dot(parts, taller, preferred_element_type=F32)
                value = jnp.sum(jnp.where(at_row, seen, 0.0), axis=0, keepdims=True)
                misfit = value - obs_ref[pol, ri, comp : comp + 1, :]
                weight = wt_ref[pol, comp : comp + 1, :]
                weighted = weight * weight * misfit
                data[1, p : p + 1, :] = weighted if ri == 0 else -weighted

    data_up = remote(data.at[1], data.at[0], data_send.at[0], data_recv.at[0], above_to)
    data_down = remote(data.at[1], data.at[2], data_send.at[1], data_recv.at[1], below_to)

    @pl.when(has_above)
    def _():
        data_up.start()
        for c in ups:
            c.wait_send()

    @pl.when(has_below)
    def _():
        data_down.start()
        for c in downs:
            c.wait_send()

    prior_copy.wait()
    prior_all[place] = prior_pair[...]
    fan = []
    for d in range(1, positions):
        to = (base + (place + d) % positions, slab)
        fan.append(
            remote(prior_pair, prior_all.at[place], fan_send.at[0, d], fan_recv.at[0, place], to)
        )
    for c in fan:
        c.start()

    def scatter(n, first_row, count, layer_at):
        line_of, lane_of = onehots(n)
        column = (lax.broadcasted_iota(jnp.int32, (128, 128), 0) == lane_of).astype(F32)
        column = column.astype(BF16)
        wider = jnp.concatenate([column] * 3, axis=1)
        rows_here = lax.broadcasted_iota(jnp.int32, (32 * count, 128), 0) + first_row
        hit = rows_here == line_of
        for p in range(12):
            parts = split3(data[n, p : p + 1, :])
            spread = [
                jnp.where(hit, part.astype(F32), 0.0).astype(BF16) for part in parts
            ]
            placed = lax.dot_general(
                jnp.concatenate(spread, axis=1),
                wider,
                (((1,), (1,)), ((), ())),
                preferred_element_type=F32,
            )
            v0[p, layer_at : layer_at + count, 8:40, :] = placed.reshape(count, 32, 128)

    scatter(1, 0, layers, own_lo)

    @pl.when(has_below)
    def _():
        data_up.wait_recv()

    @pl.when(has_above)
    def _():
        data_down.wait_recv()

    scatter(0, 32 * (layers - LOW), LOW, 0)
    scatter(2, 0, HIGH, own_hi)

    for src, dst, grow in ((v0, v1, 2), (v1, v2, 1), (v2, v3, 0)):
        if grow:
            sweep(src, dst, own_lo - grow, own_lo, alive_low)
        sweep(src, dst, own_lo, own_hi)
        sweep(src, dst, own_hi, own_hi + grow + 1, alive_high)
    row, sent_b = slab_total(1, moment_row((v0, v1, v2, v3)))
    coefs = solve_coefficients(row)

    def write_grad(l, carry):
        for r in range(4):
            total = None
            for pol in range(2):
                for comp in range(3):
                    re, im = combined(coefs, pol, comp, l, 8 + 8 * r)
                    f_re = field[pol * 6 + comp, l - own_lo, 8 * r : 8 * r + 8, :]
                    f_im = field[pol * 6 + 3 + comp, l - own_lo, 8 * r : 8 * r + 8, :]
                    term = re * f_im + im * f_re
                    total = term if total is None else total + term
            grad[l - own_lo, 8 * r : 8 * r + 8, :] = kap[l, 8 * r : 8 * r + 8, :] * total
        return carry

    lax.fori_loop(own_lo, own_hi, write_grad, 0)

    for y in range(2 * positions):
        for l in range(layers):
            grad_src[y % positions, y // positions, l : l + 1, :] = grad[l, y : y + 1, :]
    grad_in[place] = grad_src[place]
    spread = []
    for d in range(1, positions):
        j = (place + d) % positions
        spread.append(
            remote(
                grad_src.at[j],
                grad_in.at[place],
                fan_send.at[1, d],
                fan_recv.at[1, place],
                (base + j, slab),
            )
        )
    for c in spread:
        c.start()

    def gathered(n, ref):
        for d in range(1, positions):
            j = (place + d) % positions
            remote(
                ref.at[j], ref.at[j], fan_send.at[n, d], fan_recv.at[n, j], (base + j, slab)
            ).wait_recv()

    gathered(1, grad_in)
    partial = grad_in[0]
    for j in range(1, positions):
        partial = partial + grad_in[j]
    grad_pair[half] = partial
    pair_copy = remote(
        grad_pair.at[half], grad_pair.at[half], pair_send.at[1], pair_recv.at[1], (partner, slab)
    )
    pair_copy.start()
    gathered(0, prior_all)
    pair_copy.wait_recv()
    grad_all[place] = grad_pair[0] + grad_pair[1]
    share = []
    for d in range(1, positions):
        to = (base + (place + d) % positions, slab)
        share.append(
            remote(
                grad_all.at[place], grad_all.at[place], fan_send.at[2, d], fan_recv.at[2, place], to
            )
        )
    for c in share:
        c.start()
    gathered(2, grad_all)

    sums = [None] * 5
    for j in range(positions):
        for h in range(2):
            g, q, d = grad_all[j, h], prior_all[j, h, 0], prior_all[j, h, 1]
            for n, term in enumerate((g * g, g * q, g * d, q * q, d * d)):
                sums[n] = term if sums[n] is None else sums[n] + term
    lanes = lax.broadcasted_iota(jnp.int32, (1, 128), 1)
    row = jnp.zeros((1, 128), F32)
    for n, s in enumerate(sums):
        line = jnp.sum(s, axis=0, keepdims=True)
        row = row + jnp.where(lanes == n, jnp.sum(line, axis=1, keepdims=True), 0.0)
    row, sent_c = slab_total(2, row)
    gg, gq, gd, qq, dd = [
        jnp.sum(jnp.where(lanes == n, row, 0.0), axis=1, keepdims=True) for n in range(5)
    ]
    cells = float(slabs * layers * 32 * 128)
    mean_square = gg / cells + epsilon
    inverse = 1.0 / jnp.sqrt(mean_square)
    beta = (gg / mean_square - gq * inverse) / (qq + epsilon)
    squared = gg / mean_square - 2.0 * beta * (gd * inverse) + beta * beta * dd
    norm = 1.0 / jnp.sqrt(jnp.maximum(squared, 0.0) / cells + epsilon)
    from_grad = -inverse * norm
    from_prior = beta * norm
    for j in range(positions):
        for h in range(2):
            value = from_grad * grad_all[j, h] + from_prior * prior_all[j, h, 1]
            unit[j, h] = value
    for y in range(2 * positions):
        for l in range(layers):
            natural[l, y : y + 1, :] = unit[y % positions, y // positions, l : l + 1, :]
    for l in range(layers):
        dir_ref[l] = unit[place, half, l : l + 1, :]
    trial_ref[...] = logc_ref[...] + step_ref[0] * natural[...]

    @pl.when(has_above)
    def _():
        data_up.wait_send()

    @pl.when(has_below)
    def _():
        data_down.wait_send()

    pair_copy.wait_send()
    for c in sent_a + sent_b + sent_c + fan + spread + share:
        c.wait_send()


def per_device(
    slabs,
    positions,
    log_conductivity,
    omega,
    sources,
    receivers,
    observed,
    data_weight,
    prior_gradient,
    prior_direction,
    step_length,
):
    layers = log_conductivity.shape[0]
    total = LOW + layers + HIGH
    vmem = pl.BlockSpec(memory_space=pltpu.VMEM)
    smem = pl.BlockSpec(memory_space=pltpu.SMEM)
    wide = pltpu.VMEM((12, total, 48, 128), F32)
    chunk = (positions, 2, layers, 128)
    return pl.pallas_call(
        functools.partial(kernel, layers, slabs, positions),
        out_shape=(
            jax.ShapeDtypeStruct(prior_gradient.shape, F32),
            jax.ShapeDtypeStruct(log_conductivity.shape, F32),
        ),
        in_specs=[smem, smem, vmem, pl.BlockSpec(memory_space=pl.ANY)] + [vmem] * 5,
        out_specs=(vmem, vmem),
        scratch_shapes=[
            wide,
            wide,
            wide,
            wide,
            pltpu.VMEM((12, layers, 32, 128), F32),
            pltpu.VMEM((total, 32, 128), F32),
            pltpu.VMEM((5, 32, 128), F32),
            pltpu.VMEM((3, 1, 128), jnp.int32),
            pltpu.VMEM((3, 12, 128), F32),
            pltpu.VMEM((3, slabs, 1, 128), F32),
            pltpu.VMEM((2, 2, layers, 128), F32),
            pltpu.VMEM((positions, 2, 2, layers, 128), F32),
            pltpu.VMEM((layers, 32, 128), F32),
            pltpu.VMEM(chunk, F32),
            pltpu.VMEM(chunk, F32),
            pltpu.VMEM((2, 2, layers, 128), F32),
            pltpu.VMEM(chunk, F32),
            pltpu.VMEM(chunk, F32),
            pltpu.VMEM((layers, 32, 128), F32),
            pltpu.SemaphoreType.DMA,
            pltpu.SemaphoreType.DMA((2, 6)),
            pltpu.SemaphoreType.DMA((2, 6)),
            pltpu.SemaphoreType.DMA((2,)),
            pltpu.SemaphoreType.DMA((2,)),
            pltpu.SemaphoreType.DMA((3, slabs)),
            pltpu.SemaphoreType.DMA((3, slabs)),
            pltpu.SemaphoreType.DMA((2,)),
            pltpu.SemaphoreType.DMA((2,)),
            pltpu.SemaphoreType.DMA((3, positions)),
            pltpu.SemaphoreType.DMA((3, positions)),
        ],
        compiler_params=pltpu.CompilerParams(
            collective_id=0, has_side_effects=True, vmem_limit_bytes=48 * 1024 * 1024
        ),
        name="inversion_step",
    )(
        omega,
        step_length,
        log_conductivity,
        sources.reshape(12, layers, 32, 128),
        receivers.reshape(1, 128),
        observed[0],
        data_weight[0],
        prior_gradient,
        prior_direction,
    )


def solution(mesh):
    slabs = mesh.shape["slab"]
    positions = mesh.shape["freq"] // 2
    in_specs = (
        P("slab", None, None),
        P("freq"),
        P("freq", None, None, None, "slab", None, None),
        P("slab"),
        P("freq", None, None, None, "slab"),
        P("freq", None, None, "slab"),
        P("slab", "freq", None),
        P("slab", "freq", None),
        P(),
    )
    out_specs = (P("slab", "freq", None), P("slab", None, None))
    return jax.shard_map(
        functools.partial(per_device, slabs, positions),
        mesh=mesh,
        in_specs=in_specs,
        out_specs=out_specs,
        check_vma=False,
    )
```

profile of v0, /device:TPU:1, one launch (start us, length us, event | category | flops | bytes accessed | tf_op | source)
XLA Modules:
  0.0 66.8 jit_solution(12847199261146573282)
XLA Ops:
  1.3 0.0 copy-start.6
  1.9 0.0 copy-start.5
  2.0 0.0 copy-done.6
  2.0 0.7 copy-done.5
  2.6 0.0 copy-start.2
  2.6 0.0 copy-start.3
  2.6 0.0 copy-start.4
  2.7 0.7 %copy-done.2 = f32[5,1,128]{2,1,0:T(1,128)S(1)} copy-done((f32[5,1,128]{2,1,0:T(1,128)S(1)}, f32[5,1,128]{2,1,0:T(1,128)}, u32[]{:S(2)}) %copy-start.2) | copy-done | bytes 2584
  3.3 0.0 copy-done.3
  3.3 0.0 copy-done.4
  3.3 0.0 copy-start
  3.3 1.2 %copy-done = f32[1,2,2,3,5,32,128]{6,5,4,3,2,1,0:T(8,128)S(1)} copy-done((f32[1,2,2,3,5,32,128]{6,5,4,3,2,1,0:T(8,128)S(1)}, f32[1,2,2,3,5,32,128]{6,5,4,3,2,1,0:T(8,128)}, u32[]{:S(2)}) %copy-start) | copy-done | bytes 983064
  4.5 0.0 copy-start.1
  4.5 0.9 %copy-done.1 = f32[5,32,128]{2,1,0:T(8,128)S(1)} copy-done((f32[5,32,128]{2,1,0:T(8,128)S(1)}, f32[5,32,128]{2,1,0:T(8,128)}, u32[]{:S(2)}) %copy-start.1) | copy-done | bytes 81944
  5.4 60.1 %inversion_step.1 = (f32[5,1,128]{2,1,0:T(1,128)S(1)}, f32[5,32,128]{2,1,0:T(8,128)S(1)}) custom-call(f32[1]{0:T(128)S(6)} %copy.19.omega_ref, f32[1]{0:T(128)S(6)} %copy.20.step_ref, f32[5,32,128]{2,1,0:T(8,128)S(1)} %copy-done.1, f32[12,5,32,128]{3,2,1,0:T(8,128)S(1)} %bitcast.8, s32[1,128]{1,0:T(1,128)S(1)} %bitcast.11, f32[2,2,3,128]{3,2,1,0:T(4,128)S(1)} %bitcast.9, ...), custom_call_target="tpu_custom_call" | custom-call | tf_op jit(solution)/shard_map/inversion_step/pallas_call | solution.py:648
  65.6 0.6 copy.21
  66.2 0.6 copy.22
  (2 shorter events, 0.0 us)
Async XLA Ops:
  1.3 0.7 %copy-start.6 = (f32[1,2,3,128]{3,1,2,0:T(2,128)S(1)}, f32[1,2,3,128]{3,1,2,0:T(2,128)}, u32[]{:S(2)}) copy-start(f32[1,2,3,128]{3,1,2,0:T(2,128)} %param.14) | copy-start | bytes 9220
  1.9 0.7 %copy-start.5 = (f32[1,2,2,3,128]{4,2,3,1,0:T(2,128)S(1)}, f32[1,2,2,3,128]{4,2,3,1,0:T(2,128)}, u32[]{:S(2)}) copy-start(f32[1,2,2,3,128]{4,2,3,1,0:T(2,128)} %param.13) | copy-start | bytes 18436
  2.6 0.7 %copy-start.2 = (f32[5,1,128]{2,1,0:T(1,128)S(1)}, f32[5,1,128]{2,1,0:T(1,128)}, u32[]{:S(2)}) copy-start(f32[5,1,128]{2,1,0:T(1,128)} %pg_ref.1) | copy-start | bytes 7684
  2.6 0.7 %copy-start.3 = (f32[5,1,128]{2,1,0:T(1,128)S(1)}, f32[5,1,128]{2,1,0:T(1,128)}, u32[]{:S(2)}) copy-start(f32[5,1,128]{2,1,0:T(1,128)} %pd_ref.1) | copy-start | bytes 7684
  2.6 0.7 %copy-start.4 = (s32[128]{0:T(128)S(1)}, s32[128]{0:T(128)}, u32[]{:S(2)}) copy-start(s32[128]{0:T(128)} %param.12) | copy-start | bytes 1540
  3.3 1.2 %copy-start = (f32[1,2,2,3,5,32,128]{6,5,4,3,2,1,0:T(8,128)S(1)}, f32[1,2,2,3,5,32,128]{6,5,4,3,2,1,0:T(8,128)}, u32[]{:S(2)}) copy-start(f32[1,2,2,3,5,32,128]{6,5,4,3,2,1,0:T(8,128)} %param.11) | copy-start | bytes 2949124
  4.5 0.9 %copy-start.1 = (f32[5,32,128]{2,1,0:T(8,128)S(1)}, f32[5,32,128]{2,1,0:T(8,128)}, u32[]{:S(2)}) copy-start(f32[5,32,128]{2,1,0:T(8,128)} %logc_ref.1) | copy-start | bytes 245764
where the time goes:
time: 67.1 us; the launch traced here: 66.8 us
  Pallas kernels  60.1 us (90%)
  local copies, waits for them, and re-layouts  4.67 us (7%)
  between operations  1.98 us (3%)
    pallas_call x1, Pallas kernels, per_device(): pl.pallas_call(functools.partial(kernel, layers, slabs, positions), out_s...  60.1 us
    unnamed x18, local copies, waits for them, and re-layouts  4.67 us

commit v1 on v0

v1 whole, which is shorter than its diff:
```python
import functools

import jax
import jax.numpy as jnp
from jax import lax
from jax.experimental import pallas as pl
from jax.experimental.pallas import tpu as pltpu
from jax.sharding import PartitionSpec as P


MESH = pl.DeviceIdType.MESH
epsilon = 1e-06
F32 = jnp.float32
BF16 = jnp.bfloat16
LOW = 3
HIGH = 4


def cmul(a, b):
    return a[0] * b[0] - a[1] * b[1], a[0] * b[1] + a[1] * b[0]


def cadd(a, b):
    return a[0] + b[0], a[1] + b[1]


def csub(a, b):
    return a[0] - b[0], a[1] - b[1]


def cdiv(a, b):
    modulus = b[0] * b[0] + b[1] * b[1]
    return (a[0] * b[0] + a[1] * b[1]) / modulus, (a[1] * b[0] - a[0] * b[1]) / modulus


def square_poly(p):
    out = [None] * (2 * len(p) - 1)
    for i in range(len(p)):
        for j in range(i, len(p)):
            term = cmul(p[i], p[j])
            if j > i:
                term = (term[0] + term[0], term[1] + term[1])
            out[i + j] = term if out[i + j] is None else cadd(out[i + j], term)
    return out


def against(poly, moments):
    total = None
    for c, m in zip(poly, moments):
        term = cmul(c, m)
        total = term if total is None else cadd(total, term)
    return total


def coefficients(moments, theta):
    one = (jnp.ones_like(moments[0][0]), jnp.zeros_like(moments[0][0]))
    shift = (one[0] - theta[0] * (1.0 / 6.0), -theta[1] * (1.0 / 6.0))
    steps = [csub(cmul(shift, a), b) for a, b in zip(moments, moments[1:])]
    residual, direction, rho = [one], [one], moments[0]
    solution = []
    for iteration in range(4):
        alpha = cdiv(rho, against(square_poly(direction), steps))
        moved = [cmul(alpha, c) for c in direction]
        solution = [cadd(a, b) for a, b in zip(solution, moved)] + moved[len(solution) :]
        if iteration < 3:
            kept = [csub(r, cmul(shift, m)) for r, m in zip(residual, moved)]
            residual = [kept[0]]
            residual += [cadd(kept[k + 1], moved[k]) for k in range(len(moved) - 1)]
            residual += [moved[-1]]
            rho_next = against(square_poly(residual), moments)
            beta = cdiv(rho_next, rho)
            direction = [
                cadd(residual[k], cmul(beta, direction[k])) for k in range(len(direction))
            ] + [residual[-1]]
            rho = rho_next
    return [(c[0] * 6.0 ** -(k + 1), c[1] * 6.0 ** -(k + 1)) for k, c in enumerate(solution)]


def split3(x):
    high = x.astype(BF16)
    rest = x - high.astype(F32)
    mid = rest.astype(BF16)
    low = (rest - mid.astype(F32)).astype(BF16)
    return high, mid, low


def kernel(
    layers,
    slabs,
    positions,
    omega_in,
    step_in,
    logc_in,
    src_in,
    rec_in,
    obs_in,
    wt_in,
    pg_in,
    pd_in,
    dir_ref,
    trial_ref,
    omega_ref,
    step_ref,
    logc,
    obs,
    wt,
    pg,
    pd,
    v0,
    v1,
    v2,
    v3,
    field,
    kap,
    lcg,
    recs,
    data,
    allred,
    ends,
    prior_pair,
    prior_all,
    prior,
    grad,
    grad_src,
    grad_in,
    grad_pair,
    grad_all,
    whole,
    load_sem,
    near_send,
    near_recv,
    data_send,
    data_recv,
    ar_send,
    ar_recv,
    end_send,
    end_recv,
    pair_send,
    pair_recv,
    fan_send,
    fan_recv,
):
    freq = lax.axis_index("freq")
    slab = lax.axis_index("slab")
    half = freq // positions
    place = freq % positions
    base = half * positions
    cores = 2
    chips = slabs // cores
    line = 2 * chips
    high = half * chips + slab // cores
    core = slab % cores
    own_lo, own_hi = LOW, LOW + layers
    total_layers = LOW + layers + HIGH
    wide = 32 * layers
    chunk = wide // positions

    def remote(src, dst, send, recv, to):
        return pltpu.make_async_remote_copy(
            src_ref=src, dst_ref=dst, send_sem=send, recv_sem=recv, device_id=to, device_id_type=MESH
        )

    def on_line(away, other_core):
        z = (high + away) % line
        return (z // chips) * positions + place, (z % chips) * cores + other_core

    partner = on_line(chips, core)

    loads = [
        pltpu.make_async_copy(s, d, load_sem.at[n])
        for n, (s, d) in enumerate(
            (
                (src_in, v0.at[:, pl.ds(own_lo, layers), pl.ds(8, 32), :]),
                (logc_in, logc),
                (omega_in, omega_ref),
                (rec_in, recs.at[1]),
                (pg_in, pg),
                (pd_in, pd),
                (obs_in, obs),
                (wt_in, wt),
                (step_in, step_ref),
            )
        )
    ]
    for c in loads:
        c.start()
    barrier = pltpu.get_barrier_semaphore()
    greeted = [on_line(0, 1 - core)]
    greeted += [on_line(away, c) for away in range(1, line) for c in range(cores)]
    greeted += [(base + (place + d) % positions, slab) for d in range(1, positions)]
    for to in greeted:
        pl.semaphore_signal(barrier, inc=1, device_id=to, device_id_type=MESH)

    edge = jnp.zeros((12, total_layers, 1, 128), F32)
    for v in (v0, v1, v2, v3):
        v[:, :, 7:8, :] = edge
        v[:, :, 40:41, :] = edge
    has_below = slab > 0
    has_above = slab < slabs - 1

    @pl.when(slab == 0)
    def _():
        v0[:, 0:LOW, 8:40, :] = jnp.zeros((12, LOW, 32, 128), F32)
        lcg[0:2] = jnp.zeros((2, 32, 128), F32)
        recs[0] = jnp.zeros((1, 128), jnp.int32)
        data[0] = jnp.zeros((12, 128), F32)

    @pl.when(slab == slabs - 1)
    def _():
        v0[:, own_hi:total_layers, 8:40, :] = jnp.zeros((12, HIGH, 32, 128), F32)
        lcg[2:5] = jnp.zeros((3, 32, 128), F32)
        recs[2] = jnp.zeros((1, 128), jnp.int32)
        data[2] = jnp.zeros((12, 128), F32)

    lanes = lax.broadcasted_iota(jnp.int32, (1, 128), 1)
    lane8 = lax.broadcasted_iota(jnp.int32, (8, 128), 1)
    last8 = lane8 == 127

    def in_lanes(sums):
        row = jnp.zeros((1, 128), F32)
        for n, s in enumerate(sums):
            one = jnp.sum(s, axis=0, keepdims=True)
            row = row + jnp.where(lanes == n, jnp.sum(one, axis=1, keepdims=True), 0.0)
        return row

    def pick(row, n):
        return jnp.sum(jnp.where(lanes == n, row, 0.0), axis=1, keepdims=True)

    for n in (1, 2):
        loads[n].wait()
    omega = omega_ref[0]
    kap[own_lo:own_hi] = omega * jnp.exp(logc[...])
    loads[0].wait()

    def weigh(l, acc):
        acc = list(acc)
        across = jnp.where(l == own_hi - 1, 0.0, layers / (layers - 1.0)).astype(F32)
        beyond = jnp.where(l == own_hi - 1, l, l + 1)
        for r in range(4):
            y = 8 + 8 * r
            coupling = kap[l, 8 * r : 8 * r + 8, :]
            acc[6] = acc[6] + coupling
            for pol in range(2):
                square = product = None
                for p in range(6 * pol, 6 * pol + 6):
                    here = v0[p, l, y : y + 8, :]
                    more = jnp.where(last8, 0.0, pltpu.roll(here, 127, 1))
                    more = more + v0[p, l, y + 1 : y + 9, :]
                    more = more + across * v0[p, beyond, y : y + 8, :]
                    sq, pr = here * here, here * more
                    square = sq if square is None else square + sq
                    product = pr if product is None else product + pr
                acc[3 * pol] = acc[3 * pol] + square
                acc[3 * pol + 1] = acc[3 * pol + 1] + product
                acc[3 * pol + 2] = acc[3 * pol + 2] + coupling * square
        return tuple(acc)

    weights = lax.fori_loop(own_lo, own_hi, weigh, (jnp.zeros((8, 128), F32),) * 7)

    def slab_start(n, row):
        allred[n, slab] = row
        copies = [
            remote(
                allred.at[n, slab],
                allred.at[n, slab],
                ar_send.at[n, d],
                ar_recv.at[n, slab],
                (freq, (slab + d) % slabs),
            )
            for d in range(1, slabs)
        ]
        for c in copies:
            c.start()
        return copies

    def slab_finish(n):
        for d in range(1, slabs):
            other = (slab + d) % slabs
            remote(
                allred.at[n, other],
                allred.at[n, other],
                ar_send.at[n, d],
                ar_recv.at[n, other],
                (freq, other),
            ).wait_recv()
        total = allred[n, 0]
        for j in range(1, slabs):
            total = total + allred[n, j]
        return total

    weights = in_lanes(weights)
    for n in range(3, len(loads)):
        loads[n].wait()
    pl.semaphore_wait(barrier, len(greeted))
    sent = slab_start(0, weights)

    rows = pl.ds(8, 32)
    below_to = (freq, lax.max(slab - 1, 0))
    above_to = (freq, lax.min(slab + 1, slabs - 1))
    upward = [
        (recs.at[1], recs.at[0]),
        (logc.at[pl.ds(layers - 2, 2)], lcg.at[pl.ds(0, 2)]),
    ]
    downward = [
        (recs.at[1], recs.at[2]),
        (logc.at[pl.ds(0, 3)], lcg.at[pl.ds(2, 3)]),
    ]
    for k in range(HIGH):
        if k < LOW:
            upward.append(
                (v0.at[:, own_hi - 1 - k, rows, :], v0.at[:, own_lo - 1 - k, rows, :])
            )
        downward.append((v0.at[:, own_lo + k, rows, :], v0.at[:, own_hi + k, rows, :]))
    ups = [
        remote(s, d, near_send.at[0, n], near_recv.at[0, n], above_to)
        for n, (s, d) in enumerate(upward)
    ]
    downs = [
        remote(s, d, near_send.at[1, n], near_recv.at[1, n], below_to)
        for n, (s, d) in enumerate(downward)
    ]

    @pl.when(has_above)
    def _():
        for c in ups:
            c.start()

    @pl.when(has_below)
    def _():
        for c in downs:
            c.start()

    for l in range(layers):
        prior_pair[half, 0, l : l + 1, :] = pg[l]
        prior_pair[half, 1, l : l + 1, :] = pd[l]
    prior_copy = remote(
        prior_pair.at[half], prior_pair.at[half], pair_send.at[0], pair_recv.at[0], partner
    )
    prior_copy.start()

    def arrived(n):
        if n < len(ups):

            @pl.when(has_below)
            def _():
                ups[n].wait_recv()

        @pl.when(has_above)
        def _():
            downs[n].wait_recv()

    lane = lax.broadcasted_iota(jnp.int32, (32, 128), 1)
    first_lane, last_lane = lane == 0, lane == 127
    alive_low = jnp.where(slab == 0, 0.0, 1.0).astype(F32)
    alive_high = jnp.where(slab == slabs - 1, 0.0, 1.0).astype(F32)

    def step(theta, src, dst, l, mask=None):
        def around(p):
            here = src[p, l, 8:40, :]
            total = src[p, l - 1, 8:40, :] + src[p, l + 1, 8:40, :]
            total = total + (src[p, l, 7:39, :] + src[p, l, 9:41, :])
            left = jnp.where(first_lane, 0.0, pltpu.roll(here, 1, 1))
            right = jnp.where(last_lane, 0.0, pltpu.roll(here, 127, 1))
            return here, total + (left + right)

        for pol in range(2):
            shift_re, shift_im = theta[pol]
            coupling = kap[l] + shift_im
            for comp in range(3):
                p = pol * 6 + comp
                re, around_re = around(p)
                im, around_im = around(p + 3)
                if shift_re is not None:
                    around_re = around_re - shift_re * re
                    around_im = around_im - shift_re * im
                new_re = around_re + coupling * im
                new_im = around_im - coupling * re
                if mask is not None:
                    new_re, new_im = mask * new_re, mask * new_im
                dst[p, l, 8:40, :] = new_re
                dst[p + 3, l, 8:40, :] = new_im

    def sweep(theta, src, dst, lo, hi, mask=None):
        def body(l, carry):
            step(theta, src, dst, l, mask)
            return carry

        lax.fori_loop(lo, hi, body, 0)

    def both(theta, src, dst, low, high, ghost):
        def body(n, carry):
            mask = jnp.where(n == 0, alive_low, alive_high) if ghost else None
            step(theta, src, dst, low + n * (high - low), mask)
            return carry

        lax.fori_loop(0, 2, body, 0)

    def moment_sums(theta):
        v_list = (v0, v1, v2, v3)
        sums = []
        for pol in range(2):
            shift_re, shift_im = theta[pol]

            def body(l, acc):
                acc = list(acc)

                def add(k, value):
                    acc[k] = acc[k] + value

                for r in range(4):
                    y = 8 + 8 * r
                    coupling = kap[l, 8 * r : 8 * r + 8, :] + shift_im
                    for comp in range(3):
                        p = pol * 6 + comp
                        vs = [(v[p, l, y : y + 8, :], v[p + 3, l, y : y + 8, :]) for v in v_list]
                        for k in range(4):
                            re, im = vs[k]
                            add(4 * k, (re - im) * (re + im))
                            add(4 * k + 1, re * im)
                        halves = []
                        for q in (p, p + 3):
                            here = v3[q, l, y : y + 8, :]
                            right = jnp.where(last8, 0.0, pltpu.roll(here, 127, 1))
                            more = v3[q, l, y + 1 : y + 9, :] + right
                            halves.append(more + more)
                        re, im = vs[3]
                        if shift_re is not None:
                            halves = [halves[0] - shift_re * re, halves[1] - shift_re * im]
                        after = (halves[0] + coupling * im, halves[1] - coupling * re)
                        pairs = [(vs[0], vs[1]), (vs[1], vs[2]), (vs[2], vs[3]), (vs[3], after)]
                        for k, (u, w) in enumerate(pairs):
                            add(4 * k + 2, u[0] * w[0] - u[1] * w[1])
                            add(4 * k + 3, u[0] * w[1] + u[1] * w[0])
                return tuple(acc)

            zero = jnp.zeros((8, 128), F32)
            sums += list(lax.fori_loop(own_lo, own_hi, body, (zero,) * 16))
        return sums

    def layer_pair(l, acc):
        acc = list(acc)
        for pol in range(2):
            for comp in range(3):
                for r in range(4):
                    p, y = pol * 6 + comp, 8 + 8 * r
                    u = (v3[p, l, y : y + 8, :], v3[p + 3, l, y : y + 8, :])
                    w = (v3[p, l + 1, y : y + 8, :], v3[p + 3, l + 1, y : y + 8, :])
                    acc[2 * pol] = acc[2 * pol] + (u[0] * w[0] - u[1] * w[1])
                    acc[2 * pol + 1] = acc[2 * pol + 1] + (u[0] * w[1] + u[1] * w[0])
        return tuple(acc)

    def moment_row(sums, pairs):
        sums = list(sums)
        for pol in range(2):
            for part in range(2):
                at, more = 16 * pol + 14 + part, pairs[2 * pol + part]
                sums[at] = sums[at] + (more + more)
        return in_lanes(sums)

    no_pairs = (jnp.zeros((8, 128), F32),) * 4

    def solve_coefficients(row, theta):
        found = []
        for pol in range(2):
            moments = []
            for k in range(8):
                re = pick(row, 16 * pol + 2 * k) * 6.0**-k
                im = pick(row, 16 * pol + 2 * k + 1) * 6.0**-k
                if k % 2 == 0:
                    im = im + im
                moments.append((re, im))
            most = None
            for m in moments:
                size = jnp.maximum(jnp.abs(m[0]), jnp.abs(m[1]))
                most = size if most is None else jnp.maximum(most, size)
            scale = 1.0 / most
            moments = [(m[0] * scale, m[1] * scale) for m in moments]
            found.append(coefficients(moments, theta[pol]))
        return found

    def combined(coefs, pol, comp, l, y):
        p = pol * 6 + comp
        re = im = None
        for (cr, ci), v in zip(coefs[pol], (v0, v1, v2, v3)):
            a, b = v[p, l, y : y + 8, :], v[p + 3, l, y : y + 8, :]
            tr, ti = cr * a - ci * b, cr * b + ci * a
            re, im = (tr, ti) if re is None else (re + tr, im + ti)
        return re, im

    weights = slab_finish(0)
    theta = []
    for pol in range(2):
        square = pick(weights, 3 * pol)
        theta.append(
            (
                2.0 * pick(weights, 3 * pol + 1) / square,
                -pick(weights, 3 * pol + 2) / square,
            )
        )
    mean_coupling = pick(weights, 6) / float(slabs * wide * 128)
    sweep(theta, v0, v1, own_lo + 1, own_hi - 1)
    step(theta, v1, v2, own_lo + 2)
    arrived(0)
    arrived(1)
    kap[1:3] = omega * jnp.exp(lcg[0:2])
    kap[own_hi : own_hi + 3] = omega * jnp.exp(lcg[2:5])
    arrived(2)
    both(theta, v0, v1, own_lo, own_hi - 1, False)
    both(theta, v1, v2, own_lo + 1, own_hi - 2, False)
    step(theta, v2, v3, own_lo + 2)
    arrived(3)
    both(theta, v0, v1, own_lo - 1, own_hi, True)
    both(theta, v1, v2, own_lo, own_hi - 1, False)
    both(theta, v2, v3, own_lo + 1, own_hi - 2, False)
    arrived(4)
    both(theta, v0, v1, own_lo - 2, own_hi + 1, True)
    both(theta, v1, v2, own_lo - 1, own_hi, True)
    both(theta, v2, v3, own_lo, own_hi - 1, False)
    sums = moment_sums(theta)
    pairs = lax.fori_loop(own_lo, own_hi - 1, layer_pair, no_pairs)
    arrived(5)
    step(theta, v0, v1, own_hi + 2, alive_high)
    step(theta, v1, v2, own_hi + 1, alive_high)
    step(theta, v2, v3, own_hi, alive_high)
    pairs = layer_pair(own_hi - 1, pairs)
    sent += slab_start(1, moment_row(sums, pairs))
    row = slab_finish(1)
    coefs = solve_coefficients(row, theta)

    def write_field(l, carry):
        for pol in range(2):
            for comp in range(3):
                for r in range(4):
                    re, im = combined(coefs, pol, comp, l, 8 + 8 * r)
                    field[pol * 6 + comp, l - own_lo, 8 * r : 8 * r + 8, :] = re
                    field[pol * 6 + 3 + comp, l - own_lo, 8 * r : 8 * r + 8, :] = im
        return carry

    lax.fori_loop(own_lo, own_hi, write_field, 0)

    def onehots(n):
        where = recs[n]
        column = lax.broadcasted_iota(jnp.int32, (128, 128), 0) == where % 128
        return where // 128, column.astype(F32).astype(BF16)

    line_of, column = onehots(1)
    taller = jnp.concatenate([column] * 3, axis=0)
    at_row = lax.broadcasted_iota(jnp.int32, (wide, 128), 0) == line_of
    for pol in range(2):
        for ri in range(2):
            for comp in range(3):
                p = pol * 6 + ri * 3 + comp
                plane = field[p].reshape(wide, 128)
                parts = jnp.concatenate(split3(plane), axis=1)
                seen = jnp.dot(parts, taller, preferred_element_type=F32)
                value = jnp.sum(jnp.where(at_row, seen, 0.0), axis=0, keepdims=True)
                misfit = value - obs[pol, comp, ri : ri + 1, :]
                weight = wt[comp, pol : pol + 1, :]
                weighted = weight * weight * misfit
                data[1, p : p + 1, :] = weighted if ri == 0 else -weighted

    data_up = remote(data.at[1], data.at[0], data_send.at[0], data_recv.at[0], above_to)
    data_down = remote(data.at[1], data.at[2], data_send.at[1], data_recv.at[1], below_to)

    @pl.when(has_above)
    def _():
        data_up.start()
        for c in ups:
            c.wait_send()

    @pl.when(has_below)
    def _():
        data_down.start()
        for c in downs:
            c.wait_send()

    prior_copy.wait()
    prior_all[place] = prior_pair[...]
    fan = [
        remote(
            prior_pair,
            prior_all.at[place],
            fan_send.at[0, d],
            fan_recv.at[0, place],
            (base + (place + d) % positions, slab),
        )
        for d in range(1, positions)
    ]
    for c in fan:
        c.start()

    def scatter(n, first_row, count, layer_at):
        line_of, column = onehots(n)
        wider = jnp.concatenate([column] * 3, axis=1)
        rows_here = lax.broadcasted_iota(jnp.int32, (32 * count, 128), 0) + first_row
        hit = rows_here == line_of
        for p in range(12):
            parts = split3(data[n, p : p + 1, :])
            spread = [jnp.where(hit, part.astype(F32), 0.0).astype(BF16) for part in parts]
            placed = lax.dot_general(
                jnp.concatenate(spread, axis=1),
                wider,
                (((1,), (1,)), ((), ())),
                preferred_element_type=F32,
            )
            v0[p, layer_at : layer_at + count, 8:40, :] = placed.reshape(count, 32, 128)

    behind = [(None, -mean_coupling)] * 2
    scatter(1, 0, layers, own_lo)
    sweep(behind, v0, v1, own_lo + 1, own_hi - 1)
    step(behind, v1, v2, own_lo + 2)

    @pl.when(has_below)
    def _():
        data_up.wait_recv()

    @pl.when(has_above)
    def _():
        data_down.wait_recv()

    scatter(0, 32 * (layers - LOW), LOW, 0)
    scatter(2, 0, HIGH, own_hi)
    both(behind, v0, v1, own_lo, own_hi - 1, False)
    sweep(behind, v0, v1, own_lo - 2, own_lo, alive_low)
    sweep(behind, v0, v1, own_hi, own_hi + 3, alive_high)
    both(behind, v1, v2, own_lo + 1, own_hi - 2, False)
    both(behind, v1, v2, own_lo, own_hi - 1, False)
    step(behind, v1, v2, own_lo - 1, alive_low)
    sweep(behind, v1, v2, own_hi, own_hi + 2, alive_high)
    sweep(behind, v2, v3, own_lo, own_hi)
    step(behind, v2, v3, own_hi, alive_high)
    sums = moment_sums(behind)
    pairs = lax.fori_loop(own_lo, own_hi, layer_pair, no_pairs)
    sent += slab_start(2, moment_row(sums, pairs))
    row = slab_finish(2)
    coefs = solve_coefficients(row, [(jnp.zeros_like(mean_coupling), -mean_coupling)] * 2)

    def write_grad(l, carry):
        for r in range(4):
            total = None
            for pol in range(2):
                for comp in range(3):
                    re, im = combined(coefs, pol, comp, l, 8 + 8 * r)
                    f_re = field[pol * 6 + comp, l - own_lo, 8 * r : 8 * r + 8, :]
                    f_im = field[pol * 6 + 3 + comp, l - own_lo, 8 * r : 8 * r + 8, :]
                    term = re * f_im + im * f_re
                    total = term if total is None else total + term
            at = pl.multiple_of((l - own_lo) * 32 + 8 * r, 8)
            grad[pl.ds(at, 8), :] = kap[l, 8 * r : 8 * r + 8, :] * total
        return carry

    lax.fori_loop(own_lo, own_hi, write_grad, 0)

    for j in range(positions):
        grad_src[j] = grad[chunk * j : chunk * (j + 1), :]
    grad_in[place] = grad_src[place]
    spread = []
    for d in range(1, positions):
        j = (place + d) % positions
        spread.append(
            remote(
                grad_src.at[j],
                grad_in.at[place],
                fan_send.at[1, d],
                fan_recv.at[1, place],
                (base + j, slab),
            )
        )
    for c in spread:
        c.start()

    def gathered(n, ref):
        for d in range(1, positions):
            j = (place + d) % positions
            remote(
                ref.at[j], ref.at[j], fan_send.at[n, d], fan_recv.at[n, j], (base + j, slab)
            ).wait_recv()

    gathered(0, prior_all)
    for y in range(2 * positions):
        for w in range(2):
            for l in range(layers):
                prior[w, 32 * l + y : 32 * l + y + 1, :] = prior_all[
                    y % positions, y // positions, w, l : l + 1, :
                ]
    old_grad, old_dir = prior[0], prior[1]

    def folded(x):
        total = x[0:8]
        for n in range(1, wide // 8):
            total = total + x[8 * n : 8 * n + 8]
        return total

    prior_sums = [folded(old_grad * old_grad), folded(old_dir * old_dir)]

    gathered(1, grad_in)
    partial = grad_in[0]
    for j in range(1, positions):
        partial = partial + grad_in[j]
    grad_pair[half] = partial
    pair_copy = remote(
        grad_pair.at[half], grad_pair.at[half], pair_send.at[1], pair_recv.at[1], partner
    )
    pair_copy.start()
    pair_copy.wait_recv()
    grad_all[place] = grad_pair[0] + grad_pair[1]
    share = []
    for d in range(1, positions):
        to = (base + (place + d) % positions, slab)
        share.append(
            remote(
                grad_all.at[place], grad_all.at[place], fan_send.at[2, d], fan_recv.at[2, place], to
            )
        )
    for c in share:
        c.start()
    gathered(2, grad_all)
    for j in range(positions):
        whole[chunk * j : chunk * (j + 1), :] = grad_all[j]

    g = whole[...]
    sums = [folded(g * g), folded(g * old_grad), folded(g * old_dir)] + prior_sums
    ends[slab] = in_lanes(sums)
    closing = []
    for away, other in [(0, 1 - core)] + [(a, c) for a in (1, -1, 2) for c in range(cores)]:
        n = len(closing)
        to = on_line(away, other)
        source = on_line(-away, other)[1]
        closing.append(
            (
                remote(ends.at[slab], ends.at[slab], end_send.at[n], end_recv.at[slab], to),
                remote(ends.at[source], ends.at[source], end_send.at[n], end_recv.at[source], to),
            )
        )
    for c, _ in closing:
        c.start()
    for _, c in closing:
        c.wait_recv()
    row = ends[0]
    for j in range(1, slabs):
        row = row + ends[j]
    gg, gq, gd, qq, dd = [pick(row, n) for n in range(5)]
    cells = float(slabs * wide * 128)
    mean_square = gg / cells + epsilon
    inverse = 1.0 / jnp.sqrt(mean_square)
    beta = (gg / mean_square - gq * inverse) / (qq + epsilon)
    squared = gg / mean_square - 2.0 * beta * (gd * inverse) + beta * beta * dd
    norm = 1.0 / jnp.sqrt(jnp.maximum(squared, 0.0) / cells + epsilon)
    whole[...] = (-inverse * norm) * whole[...] + (beta * norm) * prior[1]
    for l in range(layers):
        dir_ref[l] = whole[pl.ds(32 * l + freq, 1), :]
    trial_ref[...] = logc[...] + step_ref[0] * whole[...].reshape(layers, 32, 128)

    @pl.when(has_above)
    def _():
        data_up.wait_send()

    @pl.when(has_below)
    def _():
        data_down.wait_send()

    pair_copy.wait_send()
    for c in sent + fan + spread + share + [c for c, _ in closing]:
        c.wait_send()


def per_device(
    slabs,
    positions,
    log_conductivity,
    omega,
    sources,
    receivers,
    observed,
    data_weight,
    prior_gradient,
    prior_direction,
    step_length,
):
    layers = log_conductivity.shape[0]
    total = LOW + layers + HIGH
    wide = layers * 32
    chunk = (positions, wide // positions, 128)
    hbm = pl.BlockSpec(memory_space=pltpu.HBM)
    vmem = pl.BlockSpec(memory_space=pltpu.VMEM)
    state = pltpu.VMEM((12, total, 48, 128), F32)
    return pl.pallas_call(
        functools.partial(kernel, layers, slabs, positions),
        out_shape=(
            jax.ShapeDtypeStruct(prior_gradient.shape, F32),
            jax.ShapeDtypeStruct(log_conductivity.shape, F32),
        ),
        in_specs=[hbm] * 9,
        out_specs=(vmem, vmem),
        scratch_shapes=[
            pltpu.SMEM((1,), F32),
            pltpu.SMEM((1,), F32),
            pltpu.VMEM((layers, 32, 128), F32),
            pltpu.VMEM((2, 3, 2, 128), F32),
            pltpu.VMEM((3, 2, 128), F32),
            pltpu.VMEM((layers, 1, 128), F32),
            pltpu.VMEM((layers, 1, 128), F32),
            state,
            state,
            state,
            state,
            pltpu.VMEM((12, layers, 32, 128), F32),
            pltpu.VMEM((total, 32, 128), F32),
            pltpu.VMEM((5, 32, 128), F32),
            pltpu.VMEM((3, 1, 128), jnp.int32),
            pltpu.VMEM((3, 12, 128), F32),
            pltpu.VMEM((3, slabs, 1, 128), F32),
            pltpu.VMEM((slabs, 1, 128), F32),
            pltpu.VMEM((2, 2, layers, 128), F32),
            pltpu.VMEM((positions, 2, 2, layers, 128), F32),
            pltpu.VMEM((2, wide, 128), F32),
            pltpu.VMEM((wide, 128), F32),
            pltpu.VMEM(chunk, F32),
            pltpu.VMEM(chunk, F32),
            pltpu.VMEM((2,) + chunk[1:], F32),
            pltpu.VMEM(chunk, F32),
            pltpu.VMEM((wide, 128), F32),
            pltpu.SemaphoreType.DMA((9,)),
            pltpu.SemaphoreType.DMA((2, 6)),
            pltpu.SemaphoreType.DMA((2, 6)),
            pltpu.SemaphoreType.DMA((2,)),
            pltpu.SemaphoreType.DMA((2,)),
            pltpu.SemaphoreType.DMA((3, slabs)),
            pltpu.SemaphoreType.DMA((3, slabs)),
            pltpu.SemaphoreType.DMA((slabs,)),
            pltpu.SemaphoreType.DMA((slabs,)),
            pltpu.SemaphoreType.DMA((2,)),
            pltpu.SemaphoreType.DMA((2,)),
            pltpu.SemaphoreType.DMA((3, positions)),
            pltpu.SemaphoreType.DMA((3, positions)),
        ],
        compiler_params=pltpu.CompilerParams(
            collective_id=0, has_side_effects=True, vmem_limit_bytes=60 * 1024 * 1024
        ),
        name="inversion_step",
    )(
        omega,
        step_length,
        log_conductivity,
        sources.reshape(12, layers, 32, 128),
        receivers.reshape(1, 128),
        observed[0].transpose(0, 2, 1, 3),
        data_weight[0].transpose(1, 0, 2),
        prior_gradient,
        prior_direction,
    )


def solution(mesh):
    slabs = mesh.shape["slab"]
    positions = mesh.shape["freq"] // 2
    in_specs = (
        P("slab", None, None),
        P("freq"),
        P("freq", None, None, None, "slab", None, None),
        P("slab"),
        P("freq", None, None, None, "slab"),
        P("freq", None, None, "slab"),
        P("slab", "freq", None),
        P("slab", "freq", None),
        P(),
    )
    out_specs = (P("slab", "freq", None), P("slab", None, None))
    return jax.shard_map(
        functools.partial(per_device, slabs, positions),
        mesh=mesh,
        in_specs=in_specs,
        out_specs=out_specs,
        check_vma=False,
    )
```

time: 67.1 us -> 64 us (0.954)
  local copies, waits for them, and re-layouts: 4.67 us -> 2.78 us
  Pallas kernels: 60.1 us -> 59.1 us
    unnamed x18 -> x4, local copies, waits for them, and re-layouts: 4.67 us -> 2.78 us
    pallas_call x1, Pallas kernels: 60.1 us -> 59.1 us  [per_device(): pl.pallas_call(functools.partial(kernel, layers, slabs, positions), out_s...]
where the time goes in v1:
time: 64 us; the launch traced here: 63.8 us
  Pallas kernels  59.1 us (92%)
  local copies, waits for them, and re-layouts  2.78 us (4%)
  between operations  1.94 us (3%)
    pallas_call x1, Pallas kernels, per_device(): pl.pallas_call(functools.partial(kernel, layers, slabs, positions), out_s...  59.1 us
    unnamed x4, local copies, waits for them, and re-layouts  2.78 us

profile of v1, /device:TPU:1, one launch (start us, length us, event | category | flops | bytes accessed | tf_op | source)
XLA Modules:
  0.0 63.8 jit_solution(8339711687820651870)
XLA Ops:
  1.9 59.1 %inversion_step.1 = (f32[5,1,128]{2,1,0:T(1,128)}, f32[5,32,128]{2,1,0:T(8,128)}) custom-call(f32[1]{0:T(128)S(6)} %copy.13.omega_in, f32[1]{0:T(128)S(6)} %copy.14.step_in, f32[5,32,128]{2,1,0:T(8,128)} %logc_in.1, f32[12,5,32,128]{3,2,1,0:T(8,128)} %bitcast.8, s32[1,128]{1,0:T(1,128)} %bitcast.11, f32[2,3,2,128]{3,2,1,0:T(2,128)} %bitcast.9, ...), custom_call_target="tpu_custom_call" | custom-call | tf_op jit(solution)/shard_map/inversion_step/pallas_call | solution.py:787
  61.0 0.0 copy-start
  61.0 0.7 %copy-done = f32[5,1,128]{2,1,0:T(1,128)S(1)} copy-done((f32[5,1,128]{2,1,0:T(1,128)S(1)}, f32[5,1,128]{2,1,0:T(1,128)}, u32[]{:S(2)}) %copy-start) | copy-done | bytes 2584
  61.7 0.6 copy.15
  62.3 1.5 %copy.16 = f32[5,32,128]{2,1,0:T(8,128)} copy(f32[5,32,128]{2,1,0:T(8,128)} %get-tuple-element.5) | data formatting | bytes 163840
Async XLA Ops:
  61.0 0.7 %copy-start = (f32[5,1,128]{2,1,0:T(1,128)S(1)}, f32[5,1,128]{2,1,0:T(1,128)}, u32[]{:S(2)}) copy-start(f32[5,1,128]{2,1,0:T(1,128)} %get-tuple-element.4) | copy-start | bytes 7684

commit v2 on v1

--- a/solution.py
+++ b/solution.py
@@ -88,8 +88,8 @@
     layers,
     slabs,
     positions,
-    omega_in,
-    step_in,
+    omega_ref,
+    step_ref,
     logc_in,
     src_in,
     rec_in,
@@ -99,8 +99,6 @@
     pd_in,
     dir_ref,
     trial_ref,
-    omega_ref,
-    step_ref,
     logc,
     obs,
     wt,
@@ -110,11 +108,20 @@
     v1,
     v2,
     v3,
-    field,
+    u0,
+    u1,
+    u2,
+    u3,
     kap,
     lcg,
     recs,
+    wanted,
+    weights_at,
+    seen,
     data,
+    row_hot,
+    column_hot,
+    products,
     allred,
     ends,
     prior_pair,
@@ -129,8 +136,8 @@
     load_sem,
     near_send,
     near_recv,
-    data_send,
-    data_recv,
+    seen_send,
+    seen_recv,
     ar_send,
     ar_recv,
     end_send,
@@ -172,13 +179,11 @@
             (
                 (src_in, v0.at[:, pl.ds(own_lo, layers), pl.ds(8, 32), :]),
                 (logc_in, logc),
-                (omega_in, omega_ref),
                 (rec_in, recs.at[1]),
                 (pg_in, pg),
                 (pd_in, pd),
                 (obs_in, obs),
                 (wt_in, wt),
-                (step_in, step_ref),
             )
         )
     ]
@@ -192,9 +197,13 @@
         pl.semaphore_signal(barrier, inc=1, device_id=to, device_id_type=MESH)
 
     edge = jnp.zeros((12, total_layers, 1, 128), F32)
-    for v in (v0, v1, v2, v3):
-        v[:, :, 7:8, :] = edge
-        v[:, :, 40:41, :] = edge
+
+    def clear_edges(arrays):
+        for v in arrays:
+            v[:, :, 7:8, :] = edge
+            v[:, :, 40:41, :] = edge
+
+    clear_edges((v0, v1, v2, v3))
     has_below = slab > 0
     has_above = slab < slabs - 1
 
@@ -203,14 +212,18 @@
         v0[:, 0:LOW, 8:40, :] = jnp.zeros((12, LOW, 32, 128), F32)
         lcg[0:2] = jnp.zeros((2, 32, 128), F32)
         recs[0] = jnp.zeros((1, 128), jnp.int32)
-        data[0] = jnp.zeros((12, 128), F32)
+        wanted[0] = jnp.zeros((2, 2, 3, 128), F32)
+        weights_at[0] = jnp.zeros((2, 3, 128), F32)
+        seen[0] = jnp.zeros((4, 2, 2, 3, 128), F32)
 
     @pl.when(slab == slabs - 1)
     def _():
         v0[:, own_hi:total_layers, 8:40, :] = jnp.zeros((12, HIGH, 32, 128), F32)
         lcg[2:5] = jnp.zeros((3, 32, 128), F32)
         recs[2] = jnp.zeros((1, 128), jnp.int32)
-        data[2] = jnp.zeros((12, 128), F32)
+        wanted[2] = jnp.zeros((2, 2, 3, 128), F32)
+        weights_at[2] = jnp.zeros((2, 3, 128), F32)
+        seen[2] = jnp.zeros((4, 2, 2, 3, 128), F32)
 
     lanes = lax.broadcasted_iota(jnp.int32, (1, 128), 1)
     lane8 = lax.broadcasted_iota(jnp.int32, (8, 128), 1)
@@ -226,8 +239,7 @@
     def pick(row, n):
         return jnp.sum(jnp.where(lanes == n, row, 0.0), axis=1, keepdims=True)
 
-    for n in (1, 2):
-        loads[n].wait()
+    loads[1].wait()
     omega = omega_ref[0]
     kap[own_lo:own_hi] = omega * jnp.exp(logc[...])
     loads[0].wait()
@@ -289,8 +301,14 @@
         return total
 
     weights = in_lanes(weights)
-    for n in range(3, len(loads)):
+    for n in range(2, len(loads)):
         loads[n].wait()
+    for pol in range(2):
+        for comp in range(3):
+            at = slice(comp, comp + 1)
+            weights_at[1, pol, at, :] = wt[comp, pol : pol + 1, :]
+            for ri in range(2):
+                wanted[1, pol, ri, at, :] = obs[pol, comp, ri : ri + 1, :]
     pl.semaphore_wait(barrier, len(greeted))
     sent = slab_start(0, weights)
 
@@ -311,6 +329,9 @@
                 (v0.at[:, own_hi - 1 - k, rows, :], v0.at[:, own_lo - 1 - k, rows, :])
             )
         downward.append((v0.at[:, own_lo + k, rows, :], v0.at[:, own_hi + k, rows, :]))
+    for ref in (wanted, weights_at):
+        upward.append((ref.at[1], ref.at[0]))
+        downward.append((ref.at[1], ref.at[2]))
     ups = [
         remote(s, d, near_send.at[0, n], near_recv.at[0, n], above_to)
         for n, (s, d) in enumerate(upward)
@@ -338,16 +359,16 @@
     )
     prior_copy.start()
 
-    def arrived(n):
-        if n < len(ups):
-
-            @pl.when(has_below)
-            def _():
+    def arrived(from_below, from_above):
+        @pl.when(has_below)
+        def _():
+            for n in from_below:
                 ups[n].wait_recv()
 
         @pl.when(has_above)
         def _():
-            downs[n].wait_recv()
+            for n in from_above:
+                downs[n].wait_recv()
 
     lane = lax.broadcasted_iota(jnp.int32, (32, 128), 1)
     first_lane, last_lane = lane == 0, lane == 127
@@ -380,12 +401,19 @@
                 dst[p, l, 8:40, :] = new_re
                 dst[p + 3, l, 8:40, :] = new_im
 
-    def sweep(theta, src, dst, lo, hi, mask=None):
-        def body(l, carry):
-            step(theta, src, dst, l, mask)
+    def sweep(theta, src, dst, lo, hi, ghosts):
+        def body(n, carry):
+            for l in (lo + 2 * n, lo + 2 * n + 1):
+                mask = None
+                if ghosts:
+                    mask = jnp.where(l < own_lo, alive_low, 1.0)
+                    mask = jnp.where(l >= own_hi, alive_high, mask)
+                step(theta, src, dst, l, mask)
             return carry
 
-        lax.fori_loop(lo, hi, body, 0)
+        lax.fori_loop(0, (hi - lo) // 2, body, 0)
+        if (hi - lo) % 2:
+            step(theta, src, dst, hi - 1)
 
     def both(theta, src, dst, low, high, ghost):
         def body(n, carry):
@@ -395,8 +423,8 @@
 
         lax.fori_loop(0, 2, body, 0)
 
-    def moment_sums(theta):
-        v_list = (v0, v1, v2, v3)
+    def moment_sums(theta, v_list):
+        v3 = v_list[3]
         sums = []
         for pol in range(2):
             shift_re, shift_im = theta[pol]
@@ -437,7 +465,7 @@
             sums += list(lax.fori_loop(own_lo, own_hi, body, (zero,) * 16))
         return sums
 
-    def layer_pair(l, acc):
+    def layer_pair(v3, l, acc):
         acc = list(acc)
         for pol in range(2):
             for comp in range(3):
@@ -449,13 +477,12 @@
                     acc[2 * pol + 1] = acc[2 * pol + 1] + (u[0] * w[1] + u[1] * w[0])
         return tuple(acc)
 
-    def moment_row(sums, pairs):
-        sums = list(sums)
-        for pol in range(2):
-            for part in range(2):
-                at, more = 16 * pol + 14 + part, pairs[2 * pol + part]
-                sums[at] = sums[at] + (more + more)
-        return in_lanes(sums)
+    def pair_row(pairs):
+        row = in_lanes([p + p for p in pairs])
+        spread = jnp.zeros((1, 128), F32)
+        for n, at in enumerate((14, 15, 30, 31)):
+            spread = spread + jnp.where(lanes == at, pick(row, n), 0.0)
+        return spread
 
     no_pairs = (jnp.zeros((8, 128), F32),) * 4
 
@@ -478,15 +505,38 @@
             found.append(coefficients(moments, theta[pol]))
         return found
 
-    def combined(coefs, pol, comp, l, y):
+    def combined(coefs, v_list, pol, comp, l, y):
         p = pol * 6 + comp
         re = im = None
-        for (cr, ci), v in zip(coefs[pol], (v0, v1, v2, v3)):
+        for (cr, ci), v in zip(coefs[pol], v_list):
             a, b = v[p, l, y : y + 8, :], v[p + 3, l, y : y + 8, :]
             tr, ti = cr * a - ci * b, cr * b + ci * a
             re, im = (tr, ti) if re is None else (re + tr, im + ti)
         return re, im
 
+    line_of, lane_of = recs[1] // 128, recs[1] % 128
+    column = lax.broadcasted_iota(jnp.int32, (128, 128), 0) == lane_of
+    column_hot[1] = column.astype(F32).astype(BF16)
+    at_row = lax.broadcasted_iota(jnp.int32, (wide, 128), 0) == line_of
+
+    def look(j, v):
+        def body(pol, carry):
+            column = column_hot[1]
+            taller = jnp.concatenate([column] * 3, axis=0)
+            for ri in range(2):
+                for comp in range(3):
+                    plane = v[pol * 6 + ri * 3 + comp, own_lo:own_hi, 8:40, :].reshape(wide, 128)
+                    parts = jnp.concatenate(split3(plane), axis=1)
+                    found = jnp.dot(parts, taller, preferred_element_type=F32)
+                    value = jnp.sum(jnp.where(at_row, found, 0.0), axis=0, keepdims=True)
+                    seen[1, j, pol, ri, comp : comp + 1, :] = value
+            return carry
+
+        lax.fori_loop(0, 2, body, 0)
+
+    forward, backward = (v0, v1, v2, v3), (u0, u1, u2, u3)
+    clear_edges(backward)
+    look(0, v0)
     weights = slab_finish(0)
     theta = []
     for pol in range(2):
@@ -498,81 +548,55 @@
             )
         )
     mean_coupling = pick(weights, 6) / float(slabs * wide * 128)
-    sweep(theta, v0, v1, own_lo + 1, own_hi - 1)
+    sweep(theta, v0, v1, own_lo + 1, own_hi - 1, False)
     step(theta, v1, v2, own_lo + 2)
-    arrived(0)
-    arrived(1)
+    arrived((0, 1), (0, 1))
     kap[1:3] = omega * jnp.exp(lcg[0:2])
     kap[own_hi : own_hi + 3] = omega * jnp.exp(lcg[2:5])
-    arrived(2)
+    arrived((2,), (2,))
     both(theta, v0, v1, own_lo, own_hi - 1, False)
     both(theta, v1, v2, own_lo + 1, own_hi - 2, False)
     step(theta, v2, v3, own_lo + 2)
-    arrived(3)
+    look(1, v1)
+    arrived((3,), (3,))
     both(theta, v0, v1, own_lo - 1, own_hi, True)
     both(theta, v1, v2, own_lo, own_hi - 1, False)
     both(theta, v2, v3, own_lo + 1, own_hi - 2, False)
-    arrived(4)
+    look(2, v2)
+    arrived((4,), (4,))
     both(theta, v0, v1, own_lo - 2, own_hi + 1, True)
     both(theta, v1, v2, own_lo - 1, own_hi, True)
     both(theta, v2, v3, own_lo, own_hi - 1, False)
-    sums = moment_sums(theta)
-    pairs = lax.fori_loop(own_lo, own_hi - 1, layer_pair, no_pairs)
-    arrived(5)
+    pair = functools.partial(layer_pair, v3)
+    row = in_lanes(moment_sums(theta, forward))
+    pairs = lax.fori_loop(own_lo, own_hi - 1, pair, no_pairs)
+    arrived((), (5,))
     step(theta, v0, v1, own_hi + 2, alive_high)
     step(theta, v1, v2, own_hi + 1, alive_high)
     step(theta, v2, v3, own_hi, alive_high)
-    pairs = layer_pair(own_hi - 1, pairs)
-    sent += slab_start(1, moment_row(sums, pairs))
-    row = slab_finish(1)
-    coefs = solve_coefficients(row, theta)
-
-    def write_field(l, carry):
-        for pol in range(2):
-            for comp in range(3):
-                for r in range(4):
-                    re, im = combined(coefs, pol, comp, l, 8 + 8 * r)
-                    field[pol * 6 + comp, l - own_lo, 8 * r : 8 * r + 8, :] = re
-                    field[pol * 6 + 3 + comp, l - own_lo, 8 * r : 8 * r + 8, :] = im
-        return carry
-
-    lax.fori_loop(own_lo, own_hi, write_field, 0)
-
-    def onehots(n):
-        where = recs[n]
-        column = lax.broadcasted_iota(jnp.int32, (128, 128), 0) == where % 128
-        return where // 128, column.astype(F32).astype(BF16)
-
-    line_of, column = onehots(1)
-    taller = jnp.concatenate([column] * 3, axis=0)
-    at_row = lax.broadcasted_iota(jnp.int32, (wide, 128), 0) == line_of
-    for pol in range(2):
-        for ri in range(2):
-            for comp in range(3):
-                p = pol * 6 + ri * 3 + comp
-                plane = field[p].reshape(wide, 128)
-                parts = jnp.concatenate(split3(plane), axis=1)
-                seen = jnp.dot(parts, taller, preferred_element_type=F32)
-                value = jnp.sum(jnp.where(at_row, seen, 0.0), axis=0, keepdims=True)
-                misfit = value - obs[pol, comp, ri : ri + 1, :]
-                weight = wt[comp, pol : pol + 1, :]
-                weighted = weight * weight * misfit
-                data[1, p : p + 1, :] = weighted if ri == 0 else -weighted
-
-    data_up = remote(data.at[1], data.at[0], data_send.at[0], data_recv.at[0], above_to)
-    data_down = remote(data.at[1], data.at[2], data_send.at[1], data_recv.at[1], below_to)
+    sent += slab_start(1, row + pair_row(pair(own_hi - 1, pairs)))
+
+    look(3, v3)
+    seen_up = remote(seen.at[1], seen.at[0], seen_send.at[0], seen_recv.at[0], above_to)
+    seen_down = remote(seen.at[1], seen.at[2], seen_send.at[1], seen_recv.at[1], below_to)
 
     @pl.when(has_above)
     def _():
-        data_up.start()
-        for c in ups:
-            c.wait_send()
+        seen_up.start()
 
     @pl.when(has_below)
     def _():
-        data_down.start()
-        for c in downs:
-            c.wait_send()
+        seen_down.start()
+
+    spots = ((0, 32 * (layers - LOW), LOW, 0), (1, 0, layers, own_lo), (2, 0, HIGH, own_hi))
+    for n, first_row, count, layer_at in spots:
+        line_of, lane_of = recs[n] // 128, recs[n] % 128
+        if n != 1:
+            column = lax.broadcasted_iota(jnp.int32, (128, 128), 0) == lane_of
+            column_hot[n] = column.astype(F32).astype(BF16)
+        rows_here = lax.broadcasted_iota(jnp.int32, (32 * count, 128), 0) + first_row
+        hit = (rows_here == line_of).astype(F32).astype(BF16)
+        row_hot[32 * layer_at : 32 * (layer_at + count), :] = hit
 
     prior_copy.wait()
     prior_all[place] = prior_pair[...]
@@ -589,67 +613,93 @@
     for c in fan:
         c.start()
 
-    def scatter(n, first_row, count, layer_at):
-        line_of, column = onehots(n)
-        wider = jnp.concatenate([column] * 3, axis=1)
-        rows_here = lax.broadcasted_iota(jnp.int32, (32 * count, 128), 0) + first_row
-        hit = rows_here == line_of
-        for p in range(12):
-            parts = split3(data[n, p : p + 1, :])
-            spread = [jnp.where(hit, part.astype(F32), 0.0).astype(BF16) for part in parts]
-            placed = lax.dot_general(
-                jnp.concatenate(spread, axis=1),
-                wider,
-                (((1,), (1,)), ((), ())),
-                preferred_element_type=F32,
-            )
-            v0[p, layer_at : layer_at + count, 8:40, :] = placed.reshape(count, 32, 128)
-
-    behind = [(None, -mean_coupling)] * 2
-    scatter(1, 0, layers, own_lo)
-    sweep(behind, v0, v1, own_lo + 1, own_hi - 1)
-    step(behind, v1, v2, own_lo + 2)
+    arrived((5, 6), (6, 7))
 
     @pl.when(has_below)
     def _():
-        data_up.wait_recv()
+        seen_up.wait_recv()
 
     @pl.when(has_above)
     def _():
-        data_down.wait_recv()
-
-    scatter(0, 32 * (layers - LOW), LOW, 0)
-    scatter(2, 0, HIGH, own_hi)
-    both(behind, v0, v1, own_lo, own_hi - 1, False)
-    sweep(behind, v0, v1, own_lo - 2, own_lo, alive_low)
-    sweep(behind, v0, v1, own_hi, own_hi + 3, alive_high)
-    both(behind, v1, v2, own_lo + 1, own_hi - 2, False)
-    both(behind, v1, v2, own_lo, own_hi - 1, False)
-    step(behind, v1, v2, own_lo - 1, alive_low)
-    sweep(behind, v1, v2, own_hi, own_hi + 2, alive_high)
-    sweep(behind, v2, v3, own_lo, own_hi)
-    step(behind, v2, v3, own_hi, alive_high)
-    sums = moment_sums(behind)
-    pairs = lax.fori_loop(own_lo, own_hi, layer_pair, no_pairs)
-    sent += slab_start(2, moment_row(sums, pairs))
+        seen_down.wait_recv()
+
+    row = slab_finish(1)
+    coefs = solve_coefficients(row, theta)
+
+    for n in range(3):
+        for pol in range(2):
+            re = im = None
+            for j, (cr, ci) in enumerate(coefs[pol]):
+                a, b = seen[n, j, pol, 0], seen[n, j, pol, 1]
+                tr, ti = cr * a - ci * b, cr * b + ci * a
+                re, im = (tr, ti) if re is None else (re + tr, im + ti)
+            weight = weights_at[n, pol]
+            square = weight * weight
+            data[n, pol, 0] = square * (re - wanted[n, pol, 0])
+            data[n, pol, 1] = -square * (im - wanted[n, pol, 1])
+
+    for n, first_row, count, layer_at in spots:
+
+        def place_sources(pol, carry, n=n, count=count, layer_at=layer_at):
+            hit = row_hot[32 * layer_at : 32 * (layer_at + count), :]
+            wider = jnp.concatenate([column_hot[n]] * 3, axis=1)
+            for ri in range(2):
+                for comp in range(3):
+                    parts = split3(data[n, pol, ri, comp : comp + 1, :])
+                    placed = lax.dot_general(
+                        jnp.concatenate([hit * part for part in parts], axis=1),
+                        wider,
+                        (((1,), (1,)), ((), ())),
+                        preferred_element_type=F32,
+                    )
+                    p = pol * 6 + ri * 3 + comp
+                    u0[p, layer_at : layer_at + count, 8:40, :] = placed.reshape(count, 32, 128)
+            return carry
+
+        lax.fori_loop(0, 2, place_sources, 0)
+
+    behind = [(None, -mean_coupling)] * 2
+    sweep(behind, u0, u1, own_lo - 2, own_hi + 3, True)
+    sweep(behind, u1, u2, own_lo - 1, own_hi + 2, True)
+    sweep(behind, u2, u3, own_lo, own_hi + 1, True)
+    sums = moment_sums(behind, backward)
+    pairs = lax.fori_loop(own_lo, own_hi, functools.partial(layer_pair, u3), no_pairs)
+    for pol in range(2):
+        for part in range(2):
+            at, more = 16 * pol + 14 + part, pairs[2 * pol + part]
+            sums[at] = sums[at] + (more + more)
+    sent += slab_start(2, in_lanes(sums))
+
+    def multiply(l, carry):
+        for r in range(4):
+            y = 8 + 8 * r
+            at = pl.multiple_of((l - own_lo) * 32 + 8 * r, 8)
+            coupling = kap[l, 8 * r : 8 * r + 8, :]
+            for pol in range(2):
+                fields = [combined(coefs, forward, pol, comp, l, y) for comp in range(3)]
+                for j, u in enumerate(backward):
+                    first = second = None
+                    for comp in range(3):
+                        p = pol * 6 + comp
+                        re, im = u[p, l, y : y + 8, :], u[p + 3, l, y : y + 8, :]
+                        f_re, f_im = fields[comp]
+                        x, z = re * f_im + im * f_re, re * f_re - im * f_im
+                        first, second = (x, z) if first is None else (first + x, second + z)
+                    products[pol, j, 0, pl.ds(at, 8), :] = coupling * first
+                    products[pol, j, 1, pl.ds(at, 8), :] = coupling * second
+        return carry
+
+    lax.fori_loop(own_lo, own_hi, multiply, 0)
     row = slab_finish(2)
     coefs = solve_coefficients(row, [(jnp.zeros_like(mean_coupling), -mean_coupling)] * 2)
-
-    def write_grad(l, carry):
-        for r in range(4):
-            total = None
-            for pol in range(2):
-                for comp in range(3):
-                    re, im = combined(coefs, pol, comp, l, 8 + 8 * r)
-                    f_re = field[pol * 6 + comp, l - own_lo, 8 * r : 8 * r + 8, :]
-                    f_im = field[pol * 6 + 3 + comp, l - own_lo, 8 * r : 8 * r + 8, :]
-                    term = re * f_im + im * f_re
+    for n in range(wide // 8):
+        total = None
+        for pol in range(2):
+            for j in range(4):
+                for part in range(2):
+                    term = coefs[pol][j][part] * products[pol, j, part, 8 * n : 8 * n + 8, :]
                     total = term if total is None else total + term
-            at = pl.multiple_of((l - own_lo) * 32 + 8 * r, 8)
-            grad[pl.ds(at, 8), :] = kap[l, 8 * r : 8 * r + 8, :] * total
-        return carry
-
-    lax.fori_loop(own_lo, own_hi, write_grad, 0)
+        grad[8 * n : 8 * n + 8, :] = total
 
     for j in range(positions):
         grad_src[j] = grad[chunk * j : chunk * (j + 1), :]
@@ -753,11 +803,13 @@
 
     @pl.when(has_above)
     def _():
-        data_up.wait_send()
+        for c in ups + [seen_up]:
+            c.wait_send()
 
     @pl.when(has_below)
     def _():
-        data_down.wait_send()
+        for c in downs + [seen_down]:
+            c.wait_send()
 
     pair_copy.wait_send()
     for c in sent + fan + spread + share + [c for c, _ in closing]:
@@ -782,6 +834,7 @@
     wide = layers * 32
     chunk = (positions, wide // positions, 128)
     hbm = pl.BlockSpec(memory_space=pltpu.HBM)
+    smem = pl.BlockSpec(memory_space=pltpu.SMEM)
     vmem = pl.BlockSpec(memory_space=pltpu.VMEM)
     state = pltpu.VMEM((12, total, 48, 128), F32)
     return pl.pallas_call(
@@ -790,25 +843,25 @@
             jax.ShapeDtypeStruct(prior_gradient.shape, F32),
             jax.ShapeDtypeStruct(log_conductivity.shape, F32),
         ),
-        in_specs=[hbm] * 9,
+        in_specs=[smem] * 2 + [hbm] * 7,
         out_specs=(vmem, vmem),
         scratch_shapes=[
-            pltpu.SMEM((1,), F32),
-            pltpu.SMEM((1,), F32),
             pltpu.VMEM((layers, 32, 128), F32),
             pltpu.VMEM((2, 3, 2, 128), F32),
             pltpu.VMEM((3, 2, 128), F32),
             pltpu.VMEM((layers, 1, 128), F32),
             pltpu.VMEM((layers, 1, 128), F32),
-            state,
-            state,
-            state,
-            state,
-            pltpu.VMEM((12, layers, 32, 128), F32),
+            *[state] * 8,
             pltpu.VMEM((total, 32, 128), F32),
             pltpu.VMEM((5, 32, 128), F32),
             pltpu.VMEM((3, 1, 128), jnp.int32),
-            pltpu.VMEM((3, 12, 128), F32),
+            pltpu.VMEM((3, 2, 2, 3, 128), F32),
+            pltpu.VMEM((3, 2, 3, 128), F32),
+            pltpu.VMEM((3, 4, 2, 2, 3, 128), F32),
+            pltpu.VMEM((3, 2, 2, 3, 128), F32),
+            pltpu.VMEM((32 * total, 128), BF16),
+            pltpu.VMEM((3, 128, 128), BF16),
+            pltpu.VMEM((2, 4, 2, wide, 128), F32),
             pltpu.VMEM((3, slabs, 1, 128), F32),
             pltpu.VMEM((slabs, 1, 128), F32),
             pltpu.VMEM((2, 2, layers, 128), F32),
@@ -820,9 +873,9 @@
             pltpu.VMEM((2,) + chunk[1:], F32),
             pltpu.VMEM(chunk, F32),
             pltpu.VMEM((wide, 128), F32),
-            pltpu.SemaphoreType.DMA((9,)),
-            pltpu.SemaphoreType.DMA((2, 6)),
-            pltpu.SemaphoreType.DMA((2, 6)),
+            pltpu.SemaphoreType.DMA((7,)),
+            pltpu.SemaphoreType.DMA((2, 8)),
+            pltpu.SemaphoreType.DMA((2, 8)),
             pltpu.SemaphoreType.DMA((2,)),
             pltpu.SemaphoreType.DMA((2,)),
             pltpu.SemaphoreType.DMA((3, slabs)),
@@ -835,19 +888,24 @@
             pltpu.SemaphoreType.DMA((3, positions)),
         ],
         compiler_params=pltpu.CompilerParams(
-            collective_id=0, has_side_effects=True, vmem_limit_bytes=60 * 1024 * 1024
+            collective_id=0, has_side_effects=True, vmem_limit_bytes=48 * 1024 * 1024
         ),
         name="inversion_step",
     )(
         omega,
         step_length,
-        log_conductivity,
-        sources.reshape(12, layers, 32, 128),
-        receivers.reshape(1, 128),
-        observed[0].transpose(0, 2, 1, 3),
-        data_weight[0].transpose(1, 0, 2),
-        prior_gradient,
-        prior_direction,
+        *(
+            pltpu.with_memory_space_constraint(x, pltpu.HBM)
+            for x in (
+                log_conductivity,
+                sources.reshape(12, layers, 32, 128),
+                receivers.reshape(1, 128),
+                observed[0].transpose(0, 2, 1, 3),
+                data_weight[0].transpose(1, 0, 2),
+                prior_gradient,
+                prior_direction,
+            )
+        ),
     )
 
 

time: 64 us -> 59.7 us (0.933)
  Pallas kernels: 59.1 us -> 56.4 us
  local copies, waits for them, and re-layouts: 2.78 us -> 1.22 us
    pallas_call x1, Pallas kernels: 59.1 us -> 56.4 us  [per_device(): pl.pallas_call(functools.partial(kernel, layers, slabs, positions), out_s...]
    unnamed x4 -> x2, local copies, waits for them, and re-layouts: 2.78 us -> 1.22 us
where the time goes in v2:
time: 59.7 us; the launch traced here: 59.6 us
  Pallas kernels  56.4 us (94%)
  between operations  1.93 us (3%)
  local copies, waits for them, and re-layouts  1.22 us (2%)
    pallas_call x1, Pallas kernels, per_device(): pl.pallas_call(functools.partial(kernel, layers, slabs, positions), out_s...  56.4 us
    unnamed x2, local copies, waits for them, and re-layouts  1.22 us

profile of v2, /device:TPU:1, one launch (start us, length us, event | category | flops | bytes accessed | tf_op | source)
XLA Modules:
  0.0 59.6 jit_solution(10866169623776795811)
XLA Ops:
  1.9 56.4 %inversion_step.1 = (f32[5,1,128]{2,1,0:T(1,128)S(1)}, f32[5,32,128]{2,1,0:T(8,128)S(1)}) custom-call(f32[1]{0:T(128)S(6)} %copy.13.omega_ref, f32[1]{0:T(128)S(6)} %copy.14.step_ref, f32[5,32,128]{2,1,0:T(8,128)} %logc_in.1, f32[12,5,32,128]{3,2,1,0:T(8,128)} %bitcast.8, s32[1,128]{1,0:T(1,128)} %bitcast.11, f32[2,3,2,128]{3,2,1,0:T(2,128)} %bitcast.9, ...), custom_call_target="tpu_custom_call" | custom-call | tf_op jit(solution)/shard_map/inversion_step/pallas_call | solution.py:840
  58.3 0.6 copy.15
  58.9 0.6 %copy.16 = f32[5,32,128]{2,1,0:T(8,128)} copy(f32[5,32,128]{2,1,0:T(8,128)S(1)} %get-tuple-element.5) | data formatting | bytes 163840

commit v3 on v2

--- a/solution.py
+++ b/solution.py
@@ -172,6 +172,14 @@
         return (z // chips) * positions + place, (z % chips) * cores + other_core
 
     partner = on_line(chips, core)
+    side = 4
+    offsets = [(dy, dx) for dy in range(positions // side) for dx in range(side)][1:]
+    offsets.sort(key=lambda o: -sum(min(k, side - k) for k in o))
+
+    def in_plane(d):
+        dy, dx = offsets[d]
+        y = (place // side + dy) % (positions // side)
+        return y * side + (place % side + dx) % side
 
     loads = [
         pltpu.make_async_copy(s, d, load_sem.at[n])
@@ -192,7 +200,7 @@
     barrier = pltpu.get_barrier_semaphore()
     greeted = [on_line(0, 1 - core)]
     greeted += [on_line(away, c) for away in range(1, line) for c in range(cores)]
-    greeted += [(base + (place + d) % positions, slab) for d in range(1, positions)]
+    greeted += [(base + in_plane(d), slab) for d in range(positions - 1)]
     for to in greeted:
         pl.semaphore_signal(barrier, inc=1, device_id=to, device_id_type=MESH)
 
@@ -271,16 +279,20 @@
 
     def slab_start(n, row):
         allred[n, slab] = row
-        copies = [
-            remote(
-                allred.at[n, slab],
-                allred.at[n, slab],
-                ar_send.at[n, d],
-                ar_recv.at[n, slab],
-                (freq, (slab + d) % slabs),
+        copies = []
+        for d in range(slabs - 1):
+            down, up = slabs - 1 - d, d
+            down = jnp.where(down > slab, down, down - 1)
+            up = jnp.where(up < slab, up, up + 1)
+            copies.append(
+                remote(
+                    allred.at[n, slab],
+                    allred.at[n, slab],
+                    ar_send.at[n, d],
+                    ar_recv.at[n, slab],
+                    (freq, jnp.where(slab < slabs // 2, down, up)),
+                )
             )
-            for d in range(1, slabs)
-        ]
         for c in copies:
             c.start()
         return copies
@@ -606,9 +618,9 @@
             prior_all.at[place],
             fan_send.at[0, d],
             fan_recv.at[0, place],
-            (base + (place + d) % positions, slab),
+            (base + in_plane(d), slab),
         )
-        for d in range(1, positions)
+        for d in range(positions - 1)
     ]
     for c in fan:
         c.start()
@@ -705,8 +717,8 @@
         grad_src[j] = grad[chunk * j : chunk * (j + 1), :]
     grad_in[place] = grad_src[place]
     spread = []
-    for d in range(1, positions):
-        j = (place + d) % positions
+    for d in range(positions - 1):
+        j = in_plane(d)
         spread.append(
             remote(
                 grad_src.at[j],
@@ -720,8 +732,8 @@
         c.start()
 
     def gathered(n, ref):
-        for d in range(1, positions):
-            j = (place + d) % positions
+        for d in range(positions - 1):
+            j = in_plane(d)
             remote(
                 ref.at[j], ref.at[j], fan_send.at[n, d], fan_recv.at[n, j], (base + j, slab)
             ).wait_recv()
@@ -755,8 +767,8 @@
     pair_copy.wait_recv()
     grad_all[place] = grad_pair[0] + grad_pair[1]
     share = []
-    for d in range(1, positions):
-        to = (base + (place + d) % positions, slab)
+    for d in range(positions - 1):
+        to = (base + in_plane(d), slab)
         share.append(
             remote(
                 grad_all.at[place], grad_all.at[place], fan_send.at[2, d], fan_recv.at[2, place], to
@@ -772,7 +784,7 @@
     sums = [folded(g * g), folded(g * old_grad), folded(g * old_dir)] + prior_sums
     ends[slab] = in_lanes(sums)
     closing = []
-    for away, other in [(0, 1 - core)] + [(a, c) for a in (1, -1, 2) for c in range(cores)]:
+    for away, other in [(a, c) for a in (2, 1, -1) for c in range(cores)] + [(0, 1 - core)]:
         n = len(closing)
         to = on_line(away, other)
         source = on_line(-away, other)[1]

time: 59.7 us -> 59.5 us (level)
  no operation moved by 1% of the time
where the time goes in v3:
time: 59.5 us; the launch traced here: 59.4 us
  Pallas kernels  56.3 us (95%)
  between operations  1.93 us (3%)
  local copies, waits for them, and re-layouts  1.22 us (2%)
    pallas_call x1, Pallas kernels, per_device(): pl.pallas_call(functools.partial(kernel, layers, slabs, positions), out_s...  56.3 us
    unnamed x2, local copies, waits for them, and re-layouts  1.22 us

profile of v3, /device:TPU:1, one launch (start us, length us, event | category | flops | bytes accessed | tf_op | source)
XLA Modules:
  0.0 59.4 jit_solution(15417564776973219329)
XLA Ops:
  1.9 56.3 %inversion_step.1 = (f32[5,1,128]{2,1,0:T(1,128)S(1)}, f32[5,32,128]{2,1,0:T(8,128)S(1)}) custom-call(f32[1]{0:T(128)S(6)} %copy.13.omega_ref, f32[1]{0:T(128)S(6)} %copy.14.step_ref, f32[5,32,128]{2,1,0:T(8,128)} %logc_in.1, f32[12,5,32,128]{3,2,1,0:T(8,128)} %bitcast.8, s32[1,128]{1,0:T(1,128)} %bitcast.11, f32[2,3,2,128]{3,2,1,0:T(2,128)} %bitcast.9, ...), custom_call_target="tpu_custom_call" | custom-call | tf_op jit(solution)/shard_map/inversion_step/pallas_call | solution.py:852
  58.2 0.6 copy.15
  58.8 0.6 %copy.16 = f32[5,32,128]{2,1,0:T(8,128)} copy(f32[5,32,128]{2,1,0:T(8,128)S(1)} %get-tuple-element.5) | data formatting | bytes 163840

commit v4 on v3

--- a/solution.py
+++ b/solution.py
@@ -12,8 +12,7 @@
 epsilon = 1e-06
 F32 = jnp.float32
 BF16 = jnp.bfloat16
-LOW = 3
-HIGH = 4
+GHOSTS = 4
 
 
 def cmul(a, b):
@@ -157,8 +156,8 @@
     line = 2 * chips
     high = half * chips + slab // cores
     core = slab % cores
-    own_lo, own_hi = LOW, LOW + layers
-    total_layers = LOW + layers + HIGH
+    own_lo, own_hi = GHOSTS, GHOSTS + layers
+    total_layers = layers + 2 * GHOSTS
     wide = 32 * layers
     chunk = wide // positions
 
@@ -217,8 +216,8 @@
 
     @pl.when(slab == 0)
     def _():
-        v0[:, 0:LOW, 8:40, :] = jnp.zeros((12, LOW, 32, 128), F32)
-        lcg[0:2] = jnp.zeros((2, 32, 128), F32)
+        v0[:, 0:own_lo, 8:40, :] = jnp.zeros((12, GHOSTS, 32, 128), F32)
+        lcg[0:3] = jnp.zeros((3, 32, 128), F32)
         recs[0] = jnp.zeros((1, 128), jnp.int32)
         wanted[0] = jnp.zeros((2, 2, 3, 128), F32)
         weights_at[0] = jnp.zeros((2, 3, 128), F32)
@@ -226,8 +225,8 @@
 
     @pl.when(slab == slabs - 1)
     def _():
-        v0[:, own_hi:total_layers, 8:40, :] = jnp.zeros((12, HIGH, 32, 128), F32)
-        lcg[2:5] = jnp.zeros((3, 32, 128), F32)
+        v0[:, own_hi:total_layers, 8:40, :] = jnp.zeros((12, GHOSTS, 32, 128), F32)
+        lcg[3:6] = jnp.zeros((3, 32, 128), F32)
         recs[2] = jnp.zeros((1, 128), jnp.int32)
         wanted[2] = jnp.zeros((2, 2, 3, 128), F32)
         weights_at[2] = jnp.zeros((2, 3, 128), F32)
@@ -329,18 +328,20 @@
     above_to = (freq, lax.min(slab + 1, slabs - 1))
     upward = [
         (recs.at[1], recs.at[0]),
-        (logc.at[pl.ds(layers - 2, 2)], lcg.at[pl.ds(0, 2)]),
+        (logc.at[pl.ds(layers - 3, 3)], lcg.at[pl.ds(0, 3)]),
     ]
     downward = [
         (recs.at[1], recs.at[2]),
-        (logc.at[pl.ds(0, 3)], lcg.at[pl.ds(2, 3)]),
+        (logc.at[pl.ds(0, 3)], lcg.at[pl.ds(3, 3)]),
     ]
-    for k in range(HIGH):
-        if k < LOW:
-            upward.append(
-                (v0.at[:, own_hi - 1 - k, rows, :], v0.at[:, own_lo - 1 - k, rows, :])
-            )
-        downward.append((v0.at[:, own_lo + k, rows, :], v0.at[:, own_hi + k, rows, :]))
+    for k in range(GHOSTS):
+        last = k == GHOSTS - 1
+        of = pl.ds(6, 6) if last else slice(None)
+        upward.append(
+            (v0.at[of, own_hi - 1 - k, rows, :], v0.at[of, own_lo - 1 - k, rows, :])
+        )
+        of = pl.ds(0, 6) if last else slice(None)
+        downward.append((v0.at[of, own_lo + k, rows, :], v0.at[of, own_hi + k, rows, :]))
     for ref in (wanted, weights_at):
         upward.append((ref.at[1], ref.at[0]))
         downward.append((ref.at[1], ref.at[2]))
@@ -387,18 +388,25 @@
     alive_low = jnp.where(slab == 0, 0.0, 1.0).astype(F32)
     alive_high = jnp.where(slab == slabs - 1, 0.0, 1.0).astype(F32)
 
-    def step(theta, src, dst, l, mask=None):
-        def around(p):
-            here = src[p, l, 8:40, :]
-            total = src[p, l - 1, 8:40, :] + src[p, l + 1, 8:40, :]
-            total = total + (src[p, l, 7:39, :] + src[p, l, 9:41, :])
-            left = jnp.where(first_lane, 0.0, pltpu.roll(here, 1, 1))
-            right = jnp.where(last_lane, 0.0, pltpu.roll(here, 127, 1))
-            return here, total + (left + right)
-
+    def alive(l):
+        inside = jnp.where(l < own_lo, alive_low, 1.0)
+        return jnp.where(l >= own_hi, alive_high, inside)
+
+    def step(theta, src, dst, where, ghosts):
         for pol in range(2):
+            l = where[pol]
+
+            def around(p, l=l):
+                here = src[p, l, 8:40, :]
+                total = src[p, l - 1, 8:40, :] + src[p, l + 1, 8:40, :]
+                total = total + (src[p, l, 7:39, :] + src[p, l, 9:41, :])
+                left = jnp.where(first_lane, 0.0, pltpu.roll(here, 1, 1))
+                right = jnp.where(last_lane, 0.0, pltpu.roll(here, 127, 1))
+                return here, total + (left + right)
+
             shift_re, shift_im = theta[pol]
             coupling = kap[l] + shift_im
+            mask = alive(l) if ghosts else None
             for comp in range(3):
                 p = pol * 6 + comp
                 re, around_re = around(p)
@@ -413,24 +421,20 @@
                 dst[p, l, 8:40, :] = new_re
                 dst[p + 3, l, 8:40, :] = new_im
 
-    def sweep(theta, src, dst, lo, hi, ghosts):
+    def sweep(theta, src, dst, starts, count, ghosts):
         def body(n, carry):
-            for l in (lo + 2 * n, lo + 2 * n + 1):
-                mask = None
-                if ghosts:
-                    mask = jnp.where(l < own_lo, alive_low, 1.0)
-                    mask = jnp.where(l >= own_hi, alive_high, mask)
-                step(theta, src, dst, l, mask)
+            for k in range(2):
+                step(theta, src, dst, [at + 2 * n + k for at in starts], ghosts)
             return carry
 
-        lax.fori_loop(0, (hi - lo) // 2, body, 0)
-        if (hi - lo) % 2:
-            step(theta, src, dst, hi - 1)
-
-    def both(theta, src, dst, low, high, ghost):
+        lax.fori_loop(0, count // 2, body, 0)
+        if count % 2:
+            step(theta, src, dst, [at + count - 1 for at in starts], ghosts)
+
+    def both(theta, src, dst, low, high, ghosts):
         def body(n, carry):
-            mask = jnp.where(n == 0, alive_low, alive_high) if ghost else None
-            step(theta, src, dst, low + n * (high - low), mask)
+            l = low + n * (high - low)
+            step(theta, src, dst, (l, l), ghosts)
             return carry
 
         lax.fori_loop(0, 2, body, 0)
@@ -477,9 +481,10 @@
             sums += list(lax.fori_loop(own_lo, own_hi, body, (zero,) * 16))
         return sums
 
-    def layer_pair(v3, l, acc):
+    def layer_pair(v3, where, acc):
         acc = list(acc)
         for pol in range(2):
+            l = where[pol]
             for comp in range(3):
                 for r in range(4):
                     p, y = pol * 6 + comp, 8 + 8 * r
@@ -496,7 +501,11 @@
             spread = spread + jnp.where(lanes == at, pick(row, n), 0.0)
         return spread
 
-    no_pairs = (jnp.zeros((8, 128), F32),) * 4
+    def layer_pairs(v3, starts, count):
+        def body(n, acc):
+            return layer_pair(v3, [at + n for at in starts], acc)
+
+        return lax.fori_loop(0, count, body, (jnp.zeros((8, 128), F32),) * 4)
 
     def solve_coefficients(row, theta):
         found = []
@@ -560,15 +569,16 @@
             )
         )
     mean_coupling = pick(weights, 6) / float(slabs * wide * 128)
-    sweep(theta, v0, v1, own_lo + 1, own_hi - 1, False)
-    step(theta, v1, v2, own_lo + 2)
+    middle = own_lo + layers // 2
+    sweep(theta, v0, v1, (own_lo + 1,) * 2, layers - 2, False)
+    step(theta, v1, v2, (middle, middle), False)
     arrived((0, 1), (0, 1))
-    kap[1:3] = omega * jnp.exp(lcg[0:2])
-    kap[own_hi : own_hi + 3] = omega * jnp.exp(lcg[2:5])
+    kap[own_lo - 3 : own_lo] = omega * jnp.exp(lcg[0:3])
+    kap[own_hi : own_hi + 3] = omega * jnp.exp(lcg[3:6])
     arrived((2,), (2,))
     both(theta, v0, v1, own_lo, own_hi - 1, False)
     both(theta, v1, v2, own_lo + 1, own_hi - 2, False)
-    step(theta, v2, v3, own_lo + 2)
+    step(theta, v2, v3, (middle, middle), False)
     look(1, v1)
     arrived((3,), (3,))
     both(theta, v0, v1, own_lo - 1, own_hi, True)
@@ -579,14 +589,14 @@
     both(theta, v0, v1, own_lo - 2, own_hi + 1, True)
     both(theta, v1, v2, own_lo - 1, own_hi, True)
     both(theta, v2, v3, own_lo, own_hi - 1, False)
-    pair = functools.partial(layer_pair, v3)
     row = in_lanes(moment_sums(theta, forward))
-    pairs = lax.fori_loop(own_lo, own_hi - 1, pair, no_pairs)
-    arrived((), (5,))
-    step(theta, v0, v1, own_hi + 2, alive_high)
-    step(theta, v1, v2, own_hi + 1, alive_high)
-    step(theta, v2, v3, own_hi, alive_high)
-    sent += slab_start(1, row + pair_row(pair(own_hi - 1, pairs)))
+    pairs = layer_pairs(v3, (own_lo, own_lo), layers - 1)
+    arrived((5,), (5,))
+    step(theta, v0, v1, (own_hi + 2, own_lo - 3), True)
+    step(theta, v1, v2, (own_hi + 1, own_lo - 2), True)
+    step(theta, v2, v3, (own_hi, own_lo - 1), True)
+    pairs = layer_pair(v3, (own_hi - 1, own_lo - 1), pairs)
+    sent += slab_start(1, row + pair_row(pairs))
 
     look(3, v3)
     seen_up = remote(seen.at[1], seen.at[0], seen_send.at[0], seen_recv.at[0], above_to)
@@ -600,7 +610,11 @@
     def _():
         seen_down.start()
 
-    spots = ((0, 32 * (layers - LOW), LOW, 0), (1, 0, layers, own_lo), (2, 0, HIGH, own_hi))
+    spots = (
+        (0, 32 * (layers - GHOSTS), GHOSTS, 0),
+        (1, 0, layers, own_lo),
+        (2, 0, GHOSTS, own_hi),
+    )
     for n, first_row, count, layer_at in spots:
         line_of, lane_of = recs[n] // 128, recs[n] % 128
         if n != 1:
@@ -625,7 +639,7 @@
     for c in fan:
         c.start()
 
-    arrived((5, 6), (6, 7))
+    arrived((6, 7), (6, 7))
 
     @pl.when(has_below)
     def _():
@@ -650,32 +664,37 @@
             data[n, pol, 0] = square * (re - wanted[n, pol, 0])
             data[n, pol, 1] = -square * (im - wanted[n, pol, 1])
 
-    for n, first_row, count, layer_at in spots:
-
-        def place_sources(pol, carry, n=n, count=count, layer_at=layer_at):
-            hit = row_hot[32 * layer_at : 32 * (layer_at + count), :]
-            wider = jnp.concatenate([column_hot[n]] * 3, axis=1)
+    for n, _, count, layer_at in spots:
+        wider = jnp.concatenate([column_hot[n]] * 3, axis=1)
+        for pol in range(2):
+            first, much = layer_at, count
+            if n == 2 - 2 * pol:
+                pass
+            elif n != 1:
+                much = count - 1
+                first = layer_at + (1 if n == 0 else 0)
+            hit = row_hot[32 * first : 32 * (first + much), :]
+            spread = []
             for ri in range(2):
                 for comp in range(3):
                     parts = split3(data[n, pol, ri, comp : comp + 1, :])
-                    placed = lax.dot_general(
-                        jnp.concatenate([hit * part for part in parts], axis=1),
-                        wider,
-                        (((1,), (1,)), ((), ())),
-                        preferred_element_type=F32,
-                    )
-                    p = pol * 6 + ri * 3 + comp
-                    u0[p, layer_at : layer_at + count, 8:40, :] = placed.reshape(count, 32, 128)
-            return carry
-
-        lax.fori_loop(0, 2, place_sources, 0)
+                    spread.append(jnp.concatenate([hit * part for part in parts], axis=1))
+            placed = lax.dot_general(
+                jnp.concatenate(spread, axis=0),
+                wider,
+                (((1,), (1,)), ((), ())),
+                preferred_element_type=F32,
+            )
+            u0[6 * pol : 6 * pol + 6, first : first + much, 8:40, :] = placed.reshape(
+                6, much, 32, 128
+            )
 
     behind = [(None, -mean_coupling)] * 2
-    sweep(behind, u0, u1, own_lo - 2, own_hi + 3, True)
-    sweep(behind, u1, u2, own_lo - 1, own_hi + 2, True)
-    sweep(behind, u2, u3, own_lo, own_hi + 1, True)
+    sweep(behind, u0, u1, (own_lo - 2, own_lo - 3), layers + 5, True)
+    sweep(behind, u1, u2, (own_lo - 1, own_lo - 2), layers + 3, True)
+    sweep(behind, u2, u3, (own_lo, own_lo - 1), layers + 1, True)
     sums = moment_sums(behind, backward)
-    pairs = lax.fori_loop(own_lo, own_hi, functools.partial(layer_pair, u3), no_pairs)
+    pairs = layer_pairs(u3, (own_lo, own_lo - 1), layers)
     for pol in range(2):
         for part in range(2):
             at, more = 16 * pol + 14 + part, pairs[2 * pol + part]
@@ -842,7 +861,7 @@
     step_length,
 ):
     layers = log_conductivity.shape[0]
-    total = LOW + layers + HIGH
+    total = layers + 2 * GHOSTS
     wide = layers * 32
     chunk = (positions, wide // positions, 128)
     hbm = pl.BlockSpec(memory_space=pltpu.HBM)
@@ -865,7 +884,7 @@
             pltpu.VMEM((layers, 1, 128), F32),
             *[state] * 8,
             pltpu.VMEM((total, 32, 128), F32),
-            pltpu.VMEM((5, 32, 128), F32),
+            pltpu.VMEM((6, 32, 128), F32),
             pltpu.VMEM((3, 1, 128), jnp.int32),
             pltpu.VMEM((3, 2, 2, 3, 128), F32),
             pltpu.VMEM((3, 2, 3, 128), F32),

time: 59.5 us -> 58.4 us (0.982)
  Pallas kernels: 56.3 us -> 55.1 us
    pallas_call x1, Pallas kernels: 56.3 us -> 55.1 us  [per_device(): pl.pallas_call(functools.partial(kernel, layers, slabs, positions), out_s...]
where the time goes in v4:
time: 58.4 us; the launch traced here: 58.3 us
  Pallas kernels  55.1 us (94%)
  between operations  1.93 us (3%)
  local copies, waits for them, and re-layouts  1.22 us (2%)
    pallas_call x1, Pallas kernels, per_device(): pl.pallas_call(functools.partial(kernel, layers, slabs, positions), out_s...  55.1 us
    unnamed x2, local copies, waits for them, and re-layouts  1.22 us

profile of v4, /device:TPU:1, one launch (start us, length us, event | category | flops | bytes accessed | tf_op | source)
XLA Modules:
  0.0 58.3 jit_solution(7417360928103922411)
XLA Ops:
  1.9 55.1 %inversion_step.1 = (f32[5,1,128]{2,1,0:T(1,128)S(1)}, f32[5,32,128]{2,1,0:T(8,128)S(1)}) custom-call(f32[1]{0:T(128)S(6)} %copy.13.omega_ref, f32[1]{0:T(128)S(6)} %copy.14.step_ref, f32[5,32,128]{2,1,0:T(8,128)} %logc_in.1, f32[12,5,32,128]{3,2,1,0:T(8,128)} %bitcast.8, s32[1,128]{1,0:T(1,128)} %bitcast.11, f32[2,3,2,128]{3,2,1,0:T(2,128)} %bitcast.9, ...), custom_call_target="tpu_custom_call" | custom-call | tf_op jit(solution)/shard_map/inversion_step/pallas_call | solution.py:871
  57.1 0.6 copy.15
  57.6 0.6 %copy.16 = f32[5,32,128]{2,1,0:T(8,128)} copy(f32[5,32,128]{2,1,0:T(8,128)S(1)} %get-tuple-element.5) | data formatting | bytes 163840

commit v5 on v4

--- a/solution.py
+++ b/solution.py
@@ -111,6 +111,7 @@
     u1,
     u2,
     u3,
+    sides,
     kap,
     lcg,
     recs,
@@ -126,6 +127,7 @@
     prior_pair,
     prior_all,
     prior,
+    prior_src,
     grad,
     grad_src,
     grad_in,
@@ -210,7 +212,7 @@
             v[:, :, 7:8, :] = edge
             v[:, :, 40:41, :] = edge
 
-    clear_edges((v0, v1, v2, v3))
+    clear_edges((v0,))
     has_below = slab > 0
     has_above = slab < slabs - 1
 
@@ -392,7 +394,7 @@
         inside = jnp.where(l < own_lo, alive_low, 1.0)
         return jnp.where(l >= own_hi, alive_high, inside)
 
-    def step(theta, src, dst, where, ghosts):
+    def step(theta, src, dst, where, ghosts, beside=None):
         for pol in range(2):
             l = where[pol]
 
@@ -400,6 +402,8 @@
                 here = src[p, l, 8:40, :]
                 total = src[p, l - 1, 8:40, :] + src[p, l + 1, 8:40, :]
                 total = total + (src[p, l, 7:39, :] + src[p, l, 9:41, :])
+                if beside is not None:
+                    return here, total + beside[p, l]
                 left = jnp.where(first_lane, 0.0, pltpu.roll(here, 1, 1))
                 right = jnp.where(last_lane, 0.0, pltpu.roll(here, 127, 1))
                 return here, total + (left + right)
@@ -421,23 +425,19 @@
                 dst[p, l, 8:40, :] = new_re
                 dst[p + 3, l, 8:40, :] = new_im
 
-    def sweep(theta, src, dst, starts, count, ghosts):
+    def sweep(theta, src, dst, starts, count, ghosts, beside=None):
         def body(n, carry):
             for k in range(2):
-                step(theta, src, dst, [at + 2 * n + k for at in starts], ghosts)
+                step(theta, src, dst, [at + 2 * n + k for at in starts], ghosts, beside)
             return carry
 
         lax.fori_loop(0, count // 2, body, 0)
         if count % 2:
-            step(theta, src, dst, [at + count - 1 for at in starts], ghosts)
+            step(theta, src, dst, [at + count - 1 for at in starts], ghosts, beside)
 
     def both(theta, src, dst, low, high, ghosts):
-        def body(n, carry):
-            l = low + n * (high - low)
+        for l in (low, high):
             step(theta, src, dst, (l, l), ghosts)
-            return carry
-
-        lax.fori_loop(0, 2, body, 0)
 
     def moment_sums(theta, v_list):
         v3 = v_list[3]
@@ -536,27 +536,32 @@
         return re, im
 
     line_of, lane_of = recs[1] // 128, recs[1] % 128
-    column = lax.broadcasted_iota(jnp.int32, (128, 128), 0) == lane_of
-    column_hot[1] = column.astype(F32).astype(BF16)
+
+    def columns(lane_of):
+        distance = jnp.abs(lax.broadcasted_iota(jnp.int32, (128, 128), 0) - lane_of)
+        both = jnp.concatenate([distance == 0, distance == 1], axis=0)
+        return both.astype(F32).astype(BF16)
+
+    column_hot[1] = columns(lane_of)
     at_row = lax.broadcasted_iota(jnp.int32, (wide, 128), 0) == line_of
 
     def look(j, v):
         def body(pol, carry):
-            column = column_hot[1]
+            column = column_hot[1, 0:128]
             taller = jnp.concatenate([column] * 3, axis=0)
-            for ri in range(2):
-                for comp in range(3):
-                    plane = v[pol * 6 + ri * 3 + comp, own_lo:own_hi, 8:40, :].reshape(wide, 128)
-                    parts = jnp.concatenate(split3(plane), axis=1)
-                    found = jnp.dot(parts, taller, preferred_element_type=F32)
-                    value = jnp.sum(jnp.where(at_row, found, 0.0), axis=0, keepdims=True)
-                    seen[1, j, pol, ri, comp : comp + 1, :] = value
+            planes = v[pl.ds(pol * 6, 6), own_lo:own_hi, 8:40, :].reshape(6 * wide, 128)
+            parts = jnp.concatenate(split3(planes), axis=1)
+            found = jnp.dot(parts, taller, preferred_element_type=F32)
+            for k in range(6):
+                rows = jnp.where(at_row, found[wide * k : wide * (k + 1)], 0.0)
+                value = jnp.sum(rows, axis=0, keepdims=True)
+                seen[1, j, pol, k // 3, k % 3 : k % 3 + 1, :] = value
             return carry
 
         lax.fori_loop(0, 2, body, 0)
 
     forward, backward = (v0, v1, v2, v3), (u0, u1, u2, u3)
-    clear_edges(backward)
+    clear_edges(forward[1:] + backward)
     look(0, v0)
     weights = slab_finish(0)
     theta = []
@@ -618,26 +623,10 @@
     for n, first_row, count, layer_at in spots:
         line_of, lane_of = recs[n] // 128, recs[n] % 128
         if n != 1:
-            column = lax.broadcasted_iota(jnp.int32, (128, 128), 0) == lane_of
-            column_hot[n] = column.astype(F32).astype(BF16)
+            column_hot[n] = columns(lane_of)
         rows_here = lax.broadcasted_iota(jnp.int32, (32 * count, 128), 0) + first_row
         hit = (rows_here == line_of).astype(F32).astype(BF16)
         row_hot[32 * layer_at : 32 * (layer_at + count), :] = hit
-
-    prior_copy.wait()
-    prior_all[place] = prior_pair[...]
-    fan = [
-        remote(
-            prior_pair,
-            prior_all.at[place],
-            fan_send.at[0, d],
-            fan_recv.at[0, place],
-            (base + in_plane(d), slab),
-        )
-        for d in range(positions - 1)
-    ]
-    for c in fan:
-        c.start()
 
     arrived((6, 7), (6, 7))
 
@@ -685,12 +674,12 @@
                 (((1,), (1,)), ((), ())),
                 preferred_element_type=F32,
             )
-            u0[6 * pol : 6 * pol + 6, first : first + much, 8:40, :] = placed.reshape(
-                6, much, 32, 128
-            )
+            own = slice(6 * pol, 6 * pol + 6), slice(first, first + much)
+            u0[*own, 8:40, :] = placed[:, 0:128].reshape(6, much, 32, 128)
+            sides[*own] = placed[:, 128:256].reshape(6, much, 32, 128)
 
     behind = [(None, -mean_coupling)] * 2
-    sweep(behind, u0, u1, (own_lo - 2, own_lo - 3), layers + 5, True)
+    sweep(behind, u0, u1, (own_lo - 2, own_lo - 3), layers + 5, True, sides)
     sweep(behind, u1, u2, (own_lo - 1, own_lo - 2), layers + 3, True)
     sweep(behind, u2, u3, (own_lo, own_lo - 1), layers + 1, True)
     sums = moment_sums(behind, backward)
@@ -700,6 +689,21 @@
             at, more = 16 * pol + 14 + part, pairs[2 * pol + part]
             sums[at] = sums[at] + (more + more)
     sent += slab_start(2, in_lanes(sums))
+
+    prior_copy.wait()
+    prior_all[place] = prior_pair[...]
+    fan = [
+        remote(
+            prior_pair,
+            prior_all.at[place],
+            fan_send.at[0, d],
+            fan_recv.at[0, place],
+            (base + in_plane(d), slab),
+        )
+        for d in range(positions - 1)
+    ]
+    for c in fan:
+        c.start()
 
     def multiply(l, carry):
         for r in range(4):
@@ -764,15 +768,21 @@
                 prior[w, 32 * l + y : 32 * l + y + 1, :] = prior_all[
                     y % positions, y // positions, w, l : l + 1, :
                 ]
-    old_grad, old_dir = prior[0], prior[1]
-
-    def folded(x):
-        total = x[0:8]
-        for n in range(1, wide // 8):
-            total = total + x[8 * n : 8 * n + 8]
+    for w in range(2):
+        for j in range(positions):
+            prior_src[w, j] = prior[w, chunk * j : chunk * (j + 1), :]
+
+    def over_chunks(a, b):
+        total = a[0] * b[0]
+        for j in range(1, positions):
+            total = total + a[j] * b[j]
         return total
 
-    prior_sums = [folded(old_grad * old_grad), folded(old_dir * old_dir)]
+    old_grad, old_dir = prior_src.at[0], prior_src.at[1]
+    prior_row = in_lanes(
+        [jnp.zeros((chunk, 128), F32)] * 3
+        + [over_chunks(old_grad, old_grad), over_chunks(old_dir, old_dir)]
+    )
 
     gathered(1, grad_in)
     partial = grad_in[0]
@@ -796,12 +806,9 @@
     for c in share:
         c.start()
     gathered(2, grad_all)
-    for j in range(positions):
-        whole[chunk * j : chunk * (j + 1), :] = grad_all[j]
-
-    g = whole[...]
-    sums = [folded(g * g), folded(g * old_grad), folded(g * old_dir)] + prior_sums
-    ends[slab] = in_lanes(sums)
+
+    others = (grad_all, old_grad, old_dir)
+    ends[slab] = in_lanes([over_chunks(grad_all, x) for x in others]) + prior_row
     closing = []
     for away, other in [(a, c) for a in (2, 1, -1) for c in range(cores)] + [(0, 1 - core)]:
         n = len(closing)
@@ -815,6 +822,8 @@
         )
     for c, _ in closing:
         c.start()
+    for j in range(positions):
+        whole[chunk * j : chunk * (j + 1), :] = grad_all[j]
     for _, c in closing:
         c.wait_recv()
     row = ends[0]
@@ -845,6 +854,17 @@
     pair_copy.wait_send()
     for c in sent + fan + spread + share + [c for c, _ in closing]:
         c.wait_send()
+
+
+def deliver(dir_in, trial_in, dir_out, trial_out, sems):
+    copies = [
+        pltpu.make_async_copy(dir_in, dir_out, sems.at[0]),
+        pltpu.make_async_copy(trial_in, trial_out, sems.at[1]),
+    ]
+    for c in copies:
+        c.start()
+    for c in copies:
+        c.wait()
 
 
 def per_device(
@@ -868,7 +888,7 @@
     smem = pl.BlockSpec(memory_space=pltpu.SMEM)
     vmem = pl.BlockSpec(memory_space=pltpu.VMEM)
     state = pltpu.VMEM((12, total, 48, 128), F32)
-    return pl.pallas_call(
+    results = pl.pallas_call(
         functools.partial(kernel, layers, slabs, positions),
         out_shape=(
             jax.ShapeDtypeStruct(prior_gradient.shape, F32),
@@ -883,6 +903,7 @@
             pltpu.VMEM((layers, 1, 128), F32),
             pltpu.VMEM((layers, 1, 128), F32),
             *[state] * 8,
+            pltpu.VMEM((12, total, 32, 128), F32),
             pltpu.VMEM((total, 32, 128), F32),
             pltpu.VMEM((6, 32, 128), F32),
             pltpu.VMEM((3, 1, 128), jnp.int32),
@@ -891,13 +912,14 @@
             pltpu.VMEM((3, 4, 2, 2, 3, 128), F32),
             pltpu.VMEM((3, 2, 2, 3, 128), F32),
             pltpu.VMEM((32 * total, 128), BF16),
-            pltpu.VMEM((3, 128, 128), BF16),
+            pltpu.VMEM((3, 256, 128), BF16),
             pltpu.VMEM((2, 4, 2, wide, 128), F32),
             pltpu.VMEM((3, slabs, 1, 128), F32),
             pltpu.VMEM((slabs, 1, 128), F32),
             pltpu.VMEM((2, 2, layers, 128), F32),
             pltpu.VMEM((positions, 2, 2, layers, 128), F32),
             pltpu.VMEM((2, wide, 128), F32),
+            pltpu.VMEM((2,) + chunk, F32),
             pltpu.VMEM((wide, 128), F32),
             pltpu.VMEM(chunk, F32),
             pltpu.VMEM(chunk, F32),
@@ -938,6 +960,15 @@
             )
         ),
     )
+    return pl.pallas_call(
+        deliver,
+        out_shape=tuple(jax.ShapeDtypeStruct(r.shape, F32) for r in results),
+        in_specs=[vmem] * 2,
+        out_specs=(hbm, hbm),
+        scratch_shapes=[pltpu.SemaphoreType.DMA((2,))],
+        compiler_params=pltpu.CompilerParams(vmem_limit_bytes=16 * 1024 * 1024),
+        name="deliver",
+    )(*results)
 
 
 def solution(mesh):

time: 58.4 us -> 57 us (0.976)
  local copies, waits for them, and re-layouts: 1.22 us -> 0 us
    unnamed x2 -> x0, local copies, waits for them, and re-layouts: 1.22 us -> none
    pallas_call x1, Pallas kernels: 55.1 us -> 54.2 us  [per_device(): pl.pallas_call(functools.partial(kernel, layers, slabs, positions), out_s...]
    pallas_call x0 -> x1, Pallas kernels: none -> 0.66 us  [per_device(): pl.pallas_call(deliver, out_shape=tuple((jax.ShapeDtypeStruct(r.shape, F3...]
where the time goes in v5:
time: 57 us; the launch traced here: 56.8 us
  Pallas kernels  54.9 us (96%)
  between operations  1.93 us (3%)
    pallas_call x1, Pallas kernels, per_device(): pl.pallas_call(functools.partial(kernel, layers, slabs, positions), out_s...  54.2 us

profile of v5, /device:TPU:1, one launch (start us, length us, event | category | flops | bytes accessed | tf_op | source)
XLA Modules:
  0.0 56.8 jit_solution(5547144841612320229)
XLA Ops:
  1.9 54.2 %inversion_step.1 = (f32[5,1,128]{2,1,0:T(1,128)S(1)}, f32[5,32,128]{2,1,0:T(8,128)S(1)}) custom-call(f32[1]{0:T(128)S(6)} %copy.11.omega_ref, f32[1]{0:T(128)S(6)} %copy.12.step_ref, f32[5,32,128]{2,1,0:T(8,128)} %logc_in.1, f32[12,5,32,128]{3,2,1,0:T(8,128)} %bitcast.8, s32[1,128]{1,0:T(1,128)} %bitcast.11, f32[2,3,2,128]{3,2,1,0:T(2,128)} %bitcast.9, ...), custom_call_target="tpu_custom_call" | custom-call | tf_op jit(solution)/shard_map/inversion_step/pallas_call | solution.py:891
  56.2 0.7 %deliver.1 = (f32[5,1,128]{2,1,0:T(1,128)}, f32[5,32,128]{2,1,0:T(8,128)}) custom-call(f32[5,1,128]{2,1,0:T(1,128)S(1)} %get-tuple-element.4.dir_in, f32[5,32,128]{2,1,0:T(8,128)S(1)} %get-tuple-element.5.trial_in), custom_call_target="tpu_custom_call" | custom-call | tf_op jit(solution)/shard_map/deliver/pallas_call | solution.py:963
